TPU v7x, 32 devices: a whole 2x2x4 slice. The times are simulated.
32 devices in a mesh: rows: 8 (over z, y), cols: 4 (over x, core).
Axes of the slice: x: 2, y: 2, z: 4, core: 2. Of those that a mesh axis runs over, the one named last changes fastest.
Arguments:
- factor_a: bfloat16 [16384, 48, 48], P('rows'), may hold values from -0.875 to 0.875
- factor_b: bfloat16 [16384, 48, 48], P('rows'), may hold values from -0.046875 to 0.046875
- next_factor: bfloat16 [16384, 48, 48], P(('rows', 'cols')), may hold values from -6 to 6
- sketch_leg: bfloat16 [48, 32], replicated, may hold values from -6 to 6
- sketch_rows: bfloat16 [16384, 32], P('rows', 'cols'), may hold values from -6 to 6
Outputs:
- basis: float32 [32, 16384, 48], P(None, ('rows', 'cols'))
- squeezed: float32 [32, 48], replicated
All inputs are finite; a program needn't handle non-finite values.
Results may differ from a plain program's by a relative error of at most 0.0003.
Values sent between devices are 32-bit elements; how exact they have to be, the bound alone decides.
No kernel may reach another device: no remote copies, remote signals or barrier semaphores. Data moves between devices by JAX's collectives and lax.ppermute only.
A program may use at most 128 MiB of HBM per device.

v0:
```python
import jax
import jax.numpy as jnp
from jax import lax
from jax.sharding import PartitionSpec as P


def per_device(factor_a, factor_b, next_factor, sketch_leg, sketch_rows):
    high = lax.Precision.HIGHEST
    local_rows = factor_a.shape[0]
    width = factor_a.shape[1]
    col_parts = lax.axis_size("cols")
    quarter = local_rows // col_parts
    col_index = lax.axis_index("cols")
    count = local_rows * lax.axis_size("rows") * width
    start = col_index * quarter
    far_part = jnp.einsum("sp,syk->pyk", sketch_rows, factor_b, preferred_element_type=jnp.float32)
    far = lax.psum(far_part, "rows")
    far_all = lax.all_gather(far, "cols", axis=0, tiled=True)
    own_rows = lax.dynamic_slice_in_dim(factor_a, start, quarter, 0)
    near = jnp.einsum("sxk,xp->psk", own_rows, sketch_leg, preferred_element_type=jnp.float32)
    sketch = jnp.einsum("psk,pyk->psy", near, far_all, precision=high)
    columns = sketch.shape[0]
    flat = sketch.reshape(columns, quarter * width)
    own_next = next_factor.reshape(quarter * width, width).astype(jnp.float32)
    gram_part = jnp.dot(flat, flat.T, precision=high)
    root_count = jnp.sqrt(jnp.float32(count))
    gram = lax.psum(gram_part, ("rows", "cols")) / count
    lower = jnp.linalg.cholesky(gram)
    basis = jax.scipy.linalg.solve_triangular(lower, flat, lower=True)
    squeeze_part = jnp.dot(basis, own_next, precision=high)
    squeezed = lax.psum(squeeze_part, ("rows", "cols")) / root_count
    return (basis.reshape(columns, quarter, width), squeezed)


def solution(mesh):
    return jax.shard_map(
        per_device,
        mesh=mesh,
        in_specs=(
            P("rows", None, None),
            P("rows", None, None),
            P(("rows", "cols"), None, None),
            P(),
            P("rows", "cols"),
        ),
        out_specs=(P(None, ("rows", "cols"), None), P()),
        check_vma=False,
    )
```

profile of v0, /device:TPU:0, one launch (start us, length us, event | category | flops | bytes accessed | tf_op | source)
XLA Modules:
  0.0 238.8 jit_solution(5856863479625042245)
XLA Ops:
  7.2 0.0 copy-start
  7.2 0.0 all-reduce.2.cloned.1.call-start
  7.2 0.7 copy-done
  7.9 8.9 %fusion.12 = f32[8,48,48]{2,0,1:T(8,128)} fusion(bf16[2048,48,48]{0,2,1:T(8,128)(2,1)} %param.6, bf16[2048,8]{0,1:T(8,128)(2,1)S(1)} %copy-done), kind=kOutput, calls=%fused_computation.8 | convolution fusion | flops 75497472 | bytes 9543680 | tf_op jit(solution)/shard_map/sp,syk->pyk/dot_general | solution.py:16
  16.8 0.0 copy-start.2
  16.8 0.0 all-reduce.2.cloned.1.call-update
  16.9 1.8 constant_dynamic-slice_fusion
  18.7 0.0 copy-done.2
  18.7 0.0 copy-start.1
  18.7 3.4 %fusion.6 = f32[32,512,48]{1,0,2:T(8,128)} fusion(bf16[512,48,48]{0,2,1:T(8,128)(2,1)S(1)} %constant_dynamic-slice_fusion, bf16[48,32]{0,1:T(8,128)(2,1)S(1)} %copy-done.2), kind=kOutput, calls=%fused_computation.6 | convolution fusion | flops 75497472 | bytes 5508096 | tf_op jit(solution)/shard_map/sxk,xp->psk/dot_general | solution.py:20
  22.1 0.0 copy-done.1
  22.1 5.0 %copy.27 = bf16[512,48,48]{1,0,2:T(8,128)(2,1)} copy(bf16[512,48,48]{0,2,1:T(8,128)(2,1)S(1)} %copy-done.1) | data formatting | bytes 4718592 | tf_op args[2]
  27.2 14.0 %reshape.25 = bf16[24576,48]{0,1:T(8,128)(2,1)} reshape(bf16[512,48,48]{1,0,2:T(8,128)(2,1)} %copy.27) | data formatting | bytes 4718592 | tf_op jit(solution)/shard_map/reshape | solution.py:24
  41.1 49.3 %all-reduce.2.cloned.1.call-done = f32[8,48,48]{2,0,1:T(8,128)} async-done(((f32[8,48,48]{2,0,1:T(8,128)}), f32[8,48,48]{2,0,1:T(8,128)}) %all-reduce.2.cloned.1.call-update) | async-done | bytes 73744 | tf_op jit(solution)/shard_map/psum | solution.py:17
  90.4 1.0 copy.20
  91.4 8.8 %all_gather.3 = f32[32,48,48]{2,1,0:T(8,128)S(1)} all-gather(f32[8,48,48]{2,1,0:T(8,128)S(1)} %copy.20), channel_id=1, replica_groups=mesh['rows'=8,'cols'=4] {'cols'}, dimensions={0}, use_global_device_ids=true | all-gather | bytes 368640 | tf_op jit(solution)/shard_map/all_gather | solution.py:18
  100.1 6.7 %fusion.2 = f32[32,512,48]{1,2,0:T(8,128)S(1)} fusion(f32[32,48,48]{2,1,0:T(8,128)S(1)} %all_gather.3, f32[32,512,48]{1,0,2:T(8,128)} %fusion.6), kind=kOutput, calls=%fused_computation.2 | convolution fusion | flops 452984832 | bytes 6586368 | tf_op jit(solution)/shard_map/psk,pyk->psy/dot_general | solution.py:21
  106.9 4.2 %fusion.9 = f32[32,32]{0,1:T(8,128)S(1)} fusion(f32[32,512,48]{1,2,0:T(8,128)S(1)} %fusion.2), kind=kOutput, calls=%fused_computation.7 | convolution fusion | flops 301989888 | bytes 3149824 | tf_op jit(solution)/shard_map/dot_general | solution.py:25
  111.1 4.7 %copy.26 = f32[32,512,48]{2,1,0:T(8,128)} copy(f32[32,512,48]{1,2,0:T(8,128)S(1)} %fusion.2) | data formatting | bytes 6291456 | tf_op jit(solution)/shard_map/psk,pyk->psy/dot_general | solution.py:21
  115.8 38.7 %psum.22 = f32[32,32]{0,1:T(8,128)S(1)} all-reduce(f32[32,32]{0,1:T(8,128)S(1)} %fusion.9), channel_id=1, replica_groups=mesh['rows'=8,'cols'=4] {'rows','cols'}, use_global_device_ids=true, to_apply=%region_1.0 | all-reduce | flops 1024 | bytes 8192 | tf_op jit(solution)/shard_map/psum | solution.py:27
  154.5 0.1 copy.25
  154.5 2.9 %cholesky.16 = f32[32,32]{1,0:T(8,128)S(1)} custom-call(f32[32,32]{1,0:T(8,128)S(1)} %fusion.17), custom_call_target="Cholesky" | custom-call | tf_op jit(solution)/shard_map/jit(cholesky)/cholesky | solution.py:28
  157.5 0.6 compare_reduce_fusion
  158.1 0.7 fusion.14
  158.8 2.4 %custom-call.7 = f32[1,32,32]{1,2,0:T(8,128)S(1)} custom-call(f32[1,32,32]{2,1,0:T(8,128)S(1)} %fusion.14), custom_call_target="InvertDiagBlocksLowerTriangular" | custom-call | tf_op jit(solution)/shard_map/jit(_solve_triangular)/triangular_solve | solution.py:29
  161.2 9.8 %reshape.23 = f32[32,24576]{1,0:T(8,128)} reshape(f32[32,512,48]{2,1,0:T(8,128)} %copy.26) | data formatting | bytes 6291456 | tf_op jit(solution)/shard_map/reshape | solution.py:23
  171.0 4.6 %fusion.15 = f32[32,24576]{1,0:T(8,128)S(1)} fusion(f32[32,24576]{1,0:T(8,128)} %reshape.23, f32[1,32,32]{1,2,0:T(8,128)S(1)} %custom-call.7), kind=kOutput, calls=%fused_computation.12 | convolution fusion | flops 301989888 | bytes 6295552 | tf_op jit(solution)/shard_map/jit(_solve_triangular)/triangular_solve | solution.py:29
  175.6 5.4 %reshape.24 = f32[32,512,48]{2,1,0:T(8,128)} reshape(f32[32,24576]{1,0:T(8,128)S(1)} %fusion.15) | data formatting | bytes 6291456 | tf_op jit(solution)/shard_map/reshape | solution.py:32
  181.0 3.7 %fusion.19 = f32[32,48]{1,0:T(8,128)S(1)} fusion(f32[32,24576]{1,0:T(8,128)S(1)} %fusion.15, bf16[24576,48]{0,1:T(8,128)(2,1)} %reshape.25), kind=kOutput, calls=%fused_computation.24 | convolution fusion | flops 452984832 | bytes 5511168 | tf_op jit(solution)/shard_map/dot_general | solution.py:30
  184.7 40.1 %psum.23 = f32[32,48]{1,0:T(8,128)S(1)} all-reduce(f32[32,48]{1,0:T(8,128)S(1)} %fusion.19), channel_id=1, replica_groups=mesh['rows'=8,'cols'=4] {'rows','cols'}, use_global_device_ids=true, to_apply=%region_4.5 | all-reduce | flops 1536 | bytes 12288 | tf_op jit(solution)/shard_map/psum | solution.py:31
  224.8 0.6 broadcast_multiply_fusion
  225.5 6.5 %copy.28 = f32[32,512,48]{1,2,0:T(8,128)} copy(f32[32,512,48]{2,1,0:T(8,128)} %reshape.24) | data formatting | bytes 6291456
  (3 shorter events, 0.0 us)
Async XLA Ops:
  7.2 0.8 copy-start
  7.2 83.2 %all-reduce.2.cloned.1.call-start = ((), (), s32[]{:S(2)}) async-start(), calls=%async_computation | async-start | bytes 393216 | tf_op jit(solution)/shard_map/psum | solution.py:17
  16.8 1.9 copy-start.2
  18.7 3.4 %copy-start.1 = (bf16[512,48,48]{0,2,1:T(8,128)(2,1)S(1)}, bf16[512,48,48]{0,2,1:T(8,128)(2,1)}, u32[]{:S(2)}) copy-start(bf16[512,48,48]{0,2,1:T(8,128)(2,1)} %param.7) | copy-start | bytes 7077892
Sparse Core Ops, SparseCore 0:
  17.0 73.3 all-reduce.1
where the time goes:
time: 239 us
  blocking collectives  87.6 us (37%)
  waiting for transfers between devices  49.3 us (21%)
  local copies, waits for them, and re-layouts  48.9 us (20%)
  matrix products  31.5 us (13%)
  between operations  14.1 us (6%)
  other arithmetic  7.3 us (3%)
    psum x1, waiting for transfers between devices, per_device(): far = lax.psum(far_part, 'rows')  49.3 us
    psum x1, blocking collectives, per_device(): squeezed = lax.psum(squeeze_part, ('rows', 'cols')) / root_count  40.1 us
    psum x1, blocking collectives, per_device(): gram = lax.psum(gram_part, ('rows', 'cols')) / count  38.7 us
    reshape x1, local copies, waits for them, and re-layouts, per_device(): own_next = next_factor.reshape(quarter * width, width).astype(jnp.float32)  14 us
    unnamed x8, local copies, waits for them, and re-layouts  12.3 us
    reshape x1, local copies, waits for them, and re-layouts, per_device(): flat = sketch.reshape(columns, quarter * width)  9.77 us
    dot_general x1, matrix products, per_device(): jnp.einsum('sp,syk->pyk', sketch_rows, factor_b, preferred_element_type=j...  8.91 us
    all_gather x1, blocking collectives, per_device(): far_all = lax.all_gather(far, 'cols', axis=0, tiled=True)  8.76 us
  transfers between devices with their start and end apart: 1, of which 1 were waited for; matrix products, arithmetic and copies ran while one was open for 10% of the time, Pallas kernels for 0%

commit v1 on v0

v1 whole, which is shorter than its diff:
```python
import jax
import jax.numpy as jnp
from jax import lax
from jax.sharding import PartitionSpec as P

BOTH = ("rows", "cols")


def gather_all(value):
    parts = lax.axis_size("rows") * lax.axis_size("cols")
    return lax.all_to_all(jnp.broadcast_to(value[None], (parts,) + value.shape), BOTH, 0, 0)


def per_device(factor_a, factor_b, next_factor, sketch_leg, sketch_rows):
    high = lax.Precision.HIGHEST
    f32 = jnp.float32
    rows, cols = lax.axis_size("rows"), lax.axis_size("cols")
    local_rows, width, bond = factor_a.shape
    quarter = local_rows // cols
    start = lax.axis_index("cols") * quarter
    count = local_rows * rows * width
    a = jnp.transpose(factor_a, (1, 2, 0))
    b = jnp.transpose(factor_b, (1, 2, 0))
    nxt = jnp.transpose(next_factor, (1, 2, 0))
    far_part = jnp.einsum("sp,yks->pyk", sketch_rows, b, preferred_element_type=f32)
    own = far_part.shape[0]
    each = -(-width // rows)
    far_part = jnp.pad(far_part, ((0, 0), (0, each * rows - width), (0, 0)))
    pieces = jnp.transpose(far_part.reshape(own, rows, each, bond), (1, 0, 2, 3))
    piece = jnp.sum(lax.all_to_all(pieces.reshape(rows, -1, 128), "rows", 0, 0), axis=0)
    far = gather_all(piece).reshape(rows, cols * own, each, bond)
    far = jnp.transpose(far, (1, 0, 2, 3)).reshape(cols * own, rows * each, bond)[:, :width]
    own_a = lax.dynamic_slice_in_dim(a, start, quarter, 2)
    near = jnp.einsum("xks,xp->pks", own_a, sketch_leg, preferred_element_type=f32)
    sketch = jnp.einsum("pyk,pks->pys", far, near, precision=high)
    columns = sketch.shape[0]
    gram_part = jnp.einsum("pys,qys->pq", sketch, sketch, precision=high)
    squeeze_part = jnp.einsum("pys,yjs->pj", sketch, nxt.astype(f32), precision=high)
    both = jnp.concatenate([gram_part, squeeze_part], axis=1)
    total = jnp.sum(gather_all(both.reshape(-1, 128)), axis=0).reshape(both.shape)
    gram = total[:, :columns] / count
    lower = jnp.linalg.cholesky(gram)
    inverse = jax.scipy.linalg.solve_triangular(lower, jnp.eye(columns, dtype=f32), lower=True)
    basis = jnp.einsum("pq,qys->pys", inverse, sketch, precision=high)
    squeezed = jnp.dot(inverse, total[:, columns:], precision=high) / jnp.sqrt(jnp.float32(count))
    return jnp.transpose(basis, (0, 2, 1)), squeezed


def solution(mesh):
    return jax.shard_map(
        per_device,
        mesh=mesh,
        in_specs=(
            P("rows", None, None),
            P("rows", None, None),
            P(BOTH, None, None),
            P(),
            P("rows", "cols"),
        ),
        out_specs=(P(None, BOTH, None), P()),
        check_vma=False,
    )
```

time: 239 us -> 90.5 us (0.38)
  blocking collectives: 87.6 us -> 29.7 us
  waiting for transfers between devices: 49.3 us -> 8 us
  local copies, waits for them, and re-layouts: 48.9 us -> 8.35 us
  between operations: 14.1 us -> 0.79 us
  starting transfers between devices: 0.04 us -> 3.3 us
    psum x2 -> x0, blocking collectives: 78.8 us -> none  [the longest x1 40.1 us: per_device(): squeezed = lax.psum(squeeze_part, ('rows', 'cols')) / root_count]
    psum x1 -> x0, waiting for transfers between devices: 49.3 us -> none  [per_device(): far = lax.psum(far_part, 'rows')]
    all_to_all x0 -> x2, blocking collectives: none -> 29.7 us  [the longest x1 15.4 us: gather_all(): lax.all_to_all(jnp.broadcast_to(value[None], (parts,) + value.shape), BOT...]
    reshape x3 -> x4, local copies, waits for them, and re-layouts: 29.1 us -> 1.85 us  [the longest x1 1.57 us: per_device(): far = gather_all(piece).reshape(rows, cols * own, each, bond)]
    all_gather x1 -> x0, blocking collectives: 8.76 us -> none  [per_device(): far_all = lax.all_gather(far, 'cols', axis=0, tiled=True)]
    unnamed x8, local copies, waits for them, and re-layouts: 12.3 us -> 3.59 us
    all_to_all x0 -> x1, waiting for transfers between devices: none -> 8 us  [gather_all(): lax.all_to_all(jnp.broadcast_to(value[None], (parts,) + value.shape), BOT...]
    dot_general x5 -> x7, matrix products: 26.9 us -> 32.9 us  [the longest x1 7.16 us: per_device(): jnp.einsum('sp,yks->pyk', sketch_rows, b, preferred_element_type=f32)]
  transfers between devices with their start and end apart: 1 -> 1, of which waited for: 1 -> 1; matrix products, arithmetic and copies ran while one was open for 10% -> 6% of each run, Pallas kernels for 0% -> 0%
where the time goes in v1:
time: 90.5 us; the launch traced here: 90.1 us
  matrix products  33.1 us (37%)
  blocking collectives  29.7 us (33%)
  local copies, waits for them, and re-layouts  8.35 us (9%)
  waiting for transfers between devices  8 us (9%)
  other arithmetic  6.82 us (8%)
  starting transfers between devices  3.3 us (4%)
    all_to_all x1, blocking collectives, gather_all(): lax.all_to_all(jnp.broadcast_to(value[None], (parts,) + value.shape), BOT...  15.4 us
    all_to_all x1, blocking collectives, per_device(): lax.all_to_all(pieces.reshape(rows, -1, 128), 'rows', 0, 0)  14.2 us
    all_to_all x1, waiting for transfers between devices, gather_all(): lax.all_to_all(jnp.broadcast_to(value[None], (parts,) + value.shape), BOT...  8 us
    dot_general x1, matrix products, per_device(): jnp.einsum('sp,yks->pyk', sketch_rows, b, preferred_element_type=f32)  7.16 us
    dot_general x1, matrix products, per_device(): sketch = jnp.einsum('pyk,pks->pys', far, near, precision=high)  6.84 us
    dot_general x1, matrix products, per_device(): basis = jnp.einsum('pq,qys->pys', inverse, sketch, precision=high)  6.44 us
    dot_general x1, matrix products, per_device(): gram_part = jnp.einsum('pys,qys->pq', sketch, sketch, precision=high)  4.19 us
    dot_general x1, matrix products, per_device(): jnp.einsum('pys,yjs->pj', sketch, nxt.astype(f32), precision=high)  4.05 us
  transfers between devices with their start and end apart: 1, of which 1 were waited for; matrix products, arithmetic and copies ran while one was open for 6% of the time, Pallas kernels for 0%

profile of v1, /device:TPU:0, one launch (start us, length us, event | category | flops | bytes accessed | tf_op | source)
XLA Modules:
  0.0 90.1 jit_solution(9820949443378259485)
XLA Ops:
  0.6 0.0 copy-start
  0.6 7.2 %fusion = f32[8,48,48]{2,0,1:T(8,128)S(1)} fusion(bf16[2048,48,48]{0,2,1:T(8,128)(2,1)} %param.6, bf16[2048,8]{0,1:T(8,128)(2,1)} %param.9), kind=kOutput, calls=%fused_computation | convolution fusion | flops 75497472 | bytes 9543680 | tf_op jit(solution)/shard_map/sp,yks->pyk/dot_general | solution.py:25
  7.8 0.1 copy.72
  7.9 0.1 reshape.32
  8.0 0.0 copy-start.2
  8.0 14.2 %all_to_all.15 = f32[8,18,128]{2,1,0:T(8,128)S(1)} all-to-all(f32[8,18,128]{2,1,0:T(8,128)S(1)} %reshape.32), channel_id=1, replica_groups=mesh['rows'=8,'cols'=4] {'rows'}, dimensions={0} | all-to-all | bytes 147456 | tf_op jit(solution)/shard_map/all_to_all | solution.py:30
  22.3 0.8 broadcast_in_dim.7
  23.1 3.3 %all-to-all-start.1 = ((f32[32,18,128]{2,1,0:T(8,128)}), f32[32,18,128]{2,1,0:T(8,128)}, u32[]{:S(2)}, u32[]{:S(2)}) async-start(f32[32,18,128]{2,1,0:T(8,128)} %broadcast_in_dim.7), calls=%async_computation.1 | async-start | bytes 786432 | tf_op jit(solution)/shard_map/all_to_all | solution.py:11
  26.4 1.8 %constant_dynamic-slice_fusion = bf16[512,48,48]{0,2,1:T(8,128)(2,1)S(1)} fusion(bf16[2048,48,48]{0,2,1:T(8,128)(2,1)} %param.5, s32[]{:T(128)S(6)} %select_n.7), kind=kLoop, calls=%fused_computation.36 | loop fusion | bytes 4718596 | tf_op jit(solution)/shard_map/dynamic-slice
  28.2 0.0 copy-done.2
  28.2 3.4 %fusion.12 = f32[32,48,512]{2,0,1:T(8,128)} fusion(bf16[512,48,48]{0,2,1:T(8,128)(2,1)S(1)} %constant_dynamic-slice_fusion, bf16[48,32]{0,1:T(8,128)(2,1)S(1)} %copy-done.2), kind=kOutput, calls=%fused_computation.13 | convolution fusion | flops 75497472 | bytes 5508096 | tf_op jit(solution)/shard_map/xks,xp->pks/dot_general | solution.py:34
  31.6 8.0 %all-to-all-done.1 = f32[32,18,128]{2,1,0:T(8,128)} async-done(((f32[32,18,128]{2,1,0:T(8,128)}), f32[32,18,128]{2,1,0:T(8,128)}, u32[]{:S(2)}, u32[]{:S(2)}) %all-to-all-start.1) | async-done | bytes 294944 | tf_op jit(solution)/shard_map/all_to_all | solution.py:11
  39.6 1.6 %reshape.33 = f32[8,32,6,48]{3,2,1,0:T(8,128)S(1)} reshape(f32[32,18,128]{2,1,0:T(8,128)} %all-to-all-done.1) | data formatting | bytes 589824 | tf_op jit(solution)/shard_map/reshape | solution.py:31
  41.2 0.1 copy.36
  41.3 6.8 %fusion.2 = f32[32,48,512]{2,1,0:T(8,128)S(1)} fusion(f32[32,48,512]{2,0,1:T(8,128)} %fusion.12, f32[32,48,48]{2,0,1:T(8,128)S(1)} %bitcast.48), kind=kOutput, calls=%fused_computation.2 | convolution fusion | flops 452984832 | bytes 6586368 | tf_op jit(solution)/shard_map/pyk,pks->pys/dot_general | solution.py:35
  48.2 0.0 copy-start.1
  48.2 4.2 %fusion.21 = f32[32,32]{1,0:T(8,128)S(1)} fusion(f32[32,48,512]{2,1,0:T(8,128)S(1)} %fusion.2), kind=kOutput, calls=%fused_computation.16 | convolution fusion | flops 301989888 | bytes 3149824 | tf_op jit(solution)/shard_map/pys,qys->pq/dot_general | solution.py:37
  52.4 0.0 copy-done
  52.4 4.1 %fusion.16 = f32[32,48]{1,0:T(8,128)S(1)} fusion(bf16[512,48,48]{0,2,1:T(8,128)(2,1)S(1)} %copy-done, f32[32,48,512]{2,1,0:T(8,128)S(1)} %fusion.2), kind=kOutput, calls=%fused_computation.15 | convolution fusion | flops 452984832 | bytes 5511168 | tf_op jit(solution)/shard_map/pys,yjs->pj/dot_general | solution.py:38
  56.5 0.0 copy-done.1
  56.5 0.1 pad_maximum_fusion
  56.6 0.1 broadcast_in_dim.16
  56.7 15.4 %all_to_all.16 = f32[32,20,128]{2,1,0:T(8,128)S(1)} all-to-all(f32[32,20,128]{2,1,0:T(8,128)S(1)} %broadcast_in_dim.17), channel_id=1, replica_groups=mesh['rows'=8,'cols'=4] {'rows','cols'}, dimensions={0} | all-to-all | bytes 655360 | tf_op jit(solution)/shard_map/all_to_all | solution.py:11
  72.1 0.1 reshape.35
  72.2 0.1 copy.50
  72.3 0.1 copy.45
  72.4 2.9 %cholesky.17 = f32[32,32]{1,0:T(8,128)S(1)} custom-call(f32[32,32]{1,0:T(8,128)S(1)} %fusion.31), custom_call_target="Cholesky" | custom-call | tf_op jit(solution)/shard_map/jit(cholesky)/cholesky | solution.py:42
  75.3 0.6 compare_reduce_fusion
  76.0 0.7 fusion.26
  76.6 2.4 %custom-call.7 = f32[1,32,32]{1,2,0:T(8,128)S(1)} custom-call(f32[1,32,32]{2,1,0:T(8,128)S(1)} %fusion.26), custom_call_target="InvertDiagBlocksLowerTriangular" | custom-call | tf_op jit(solution)/shard_map/jit(_solve_triangular)/triangular_solve | solution.py:43
  79.1 0.2 fusion.29
  79.3 0.8 convolution_multiply_fusion
  80.1 6.4 %fusion.13 = f32[32,512,48]{1,0,2:T(8,128)S(1)} fusion(f32[32,48,512]{2,1,0:T(8,128)} %copy-done.1, f32[32,32]{1,0:T(8,128)S(1)} %fusion.29), kind=kOutput, calls=%fused_computation.14 | convolution fusion | flops 301989888 | bytes 6295552 | tf_op jit(solution)/shard_map/pq,qys->pys/dot_general | solution.py:44
  86.6 3.5 %copy.47 = f32[32,512,48]{1,2,0:T(8,128)} copy(f32[32,512,48]{1,0,2:T(8,128)S(1)} %fusion.13) | data formatting | bytes 6291456
  (6 shorter events, 0.1 us)
Async XLA Ops:
  0.6 51.8 %copy-start = (bf16[512,48,48]{0,2,1:T(8,128)(2,1)S(1)}, bf16[512,48,48]{0,2,1:T(8,128)(2,1)}, u32[]{:S(2)}) copy-start(bf16[512,48,48]{0,2,1:T(8,128)(2,1)} %param.7) | copy-start | bytes 7077892
  8.0 20.2 %copy-start.2 = (bf16[48,32]{0,1:T(8,128)(2,1)S(1)}, bf16[48,32]{0,1:T(8,128)(2,1)}, u32[]{:S(2)}) copy-start(bf16[48,32]{0,1:T(8,128)(2,1)} %param.8) | copy-start | bytes 9220
  23.1 16.5 %all-to-all-start.1 = ((f32[32,18,128]{2,1,0:T(8,128)}), f32[32,18,128]{2,1,0:T(8,128)}, u32[]{:S(2)}, u32[]{:S(2)}) async-start(f32[32,18,128]{2,1,0:T(8,128)} %broadcast_in_dim.7), calls=%async_computation.1 | async-start | bytes 786432 | tf_op jit(solution)/shard_map/all_to_all | solution.py:11
  48.2 8.3 %copy-start.1 = (f32[32,48,512]{2,1,0:T(8,128)}, f32[32,48,512]{2,1,0:T(8,128)S(1)}, u32[]{:S(2)}) copy-start(f32[32,48,512]{2,1,0:T(8,128)S(1)} %fusion.2) | copy-start | bytes 9437188

commit v2 on v1

v2 whole, which is shorter than its diff:
```python
import functools

import jax
import jax.numpy as jnp
from jax import lax
from jax.experimental import pallas as pl
from jax.experimental.pallas import tpu as pltpu
from jax.sharding import PartitionSpec as P

BOTH = ("rows", "cols")
F32, BF16 = jnp.float32, jnp.bfloat16
LANES = 128
VMEM = pl.BlockSpec(memory_space=pltpu.VMEM)
HBM = pl.BlockSpec(memory_space=pltpu.HBM)
NT = (((1,), (1,)), ((), ()))


def iota(shape, axis):
    return lax.broadcasted_iota(jnp.int32, shape, axis)


def halves(value):
    high = value.astype(BF16)
    return high, (value - high.astype(F32)).astype(BF16)


def params(mib):
    return pltpu.CompilerParams(vmem_limit_bytes=mib << 20)


def far_kernel(rows_ref, b_ref, a_ref, out_ref, own_ref, buf, sems, own_sem):
    pairs, used, _ = b_ref.shape
    chunks = sems.shape[0]
    step = pairs // chunks
    quarter = own_ref.shape[2]
    start = pl.multiple_of(lax.axis_index("cols") * quarter, LANES)

    def fetch(c):
        part = pl.ds(c * step, step)
        return pltpu.make_async_copy(b_ref.at[part], buf.at[part], sems.at[c])

    for c in range(chunks):
        fetch(c).start()
    own_copy = pltpu.make_async_copy(a_ref.at[:, :, pl.ds(start, quarter)], own_ref, own_sem)
    own_copy.start()
    own, lanes = out_ref.shape[1:]
    out_ref[:, :, used:] = jnp.zeros((pairs, own, lanes - used), F32)
    for c in range(chunks):
        fetch(c).wait()
        for i in range(step):
            pair = c * step + i
            out_ref[pair, :, :used] = lax.dot_general(rows_ref[...], buf[pair], NT, preferred_element_type=F32)
    own_copy.wait()


def far_sum(rows_t, b_pairs, a_t, quarter):
    pairs, used, depth = b_pairs.shape
    chunks = pairs // 2
    own = rows_t.shape[0]
    return pl.pallas_call(
        far_kernel,
        in_specs=[VMEM, HBM, HBM],
        out_specs=[VMEM, VMEM],
        out_shape=[jax.ShapeDtypeStruct((pairs, own, LANES), F32), jax.ShapeDtypeStruct(a_t.shape[:2] + (quarter,), BF16)],
        scratch_shapes=[pltpu.VMEM((pairs, used, depth), BF16), pltpu.SemaphoreType.DMA((chunks,)), pltpu.SemaphoreType.DMA],
        cost_estimate=pl.CostEstimate(flops=2 * own * pairs * used * depth, bytes_accessed=2 * pairs * used * depth, transcendentals=0),
        compiler_params=params(16),
        name="far_sum",
    )(rows_t, b_pairs, a_t)


def near_kernel(leg_ref, a_ref, high_ref, low_ref):
    columns, width = leg_ref.shape
    _, bond, quarter = a_ref.shape
    deep = 16
    wide = width * deep
    spread = (iota((width, wide), 1) // deep == iota((width, wide), 0)).astype(BF16)
    tiled = jnp.dot(leg_ref[...], spread, preferred_element_type=F32)
    tiled = jnp.broadcast_to(tiled[:, None, :], (columns, deep, wide)).reshape(columns * deep, wide)
    same = iota(tiled.shape, 1) % deep == iota(tiled.shape, 0) % deep
    weights = jnp.where(same, tiled, 0.0).astype(BF16)
    for first in range(0, bond, deep):
        part = a_ref[:, first:first + deep, :].reshape(wide, quarter)
        high, low = halves(jnp.dot(weights, part, preferred_element_type=F32))
        high_ref[:, first:first + deep, :] = high.reshape(columns, deep, quarter)
        low_ref[:, first:first + deep, :] = low.reshape(columns, deep, quarter)


def near_sums(leg_t, a_own):
    width, bond, quarter = a_own.shape
    columns = leg_t.shape[0]
    shape = jax.ShapeDtypeStruct((columns, bond, quarter), BF16)
    return pl.pallas_call(
        near_kernel,
        in_specs=[VMEM, VMEM],
        out_specs=[VMEM, VMEM],
        out_shape=[shape, shape],
        cost_estimate=pl.CostEstimate(flops=32 * columns * bond * width * quarter, bytes_accessed=2 * width * bond * quarter, transcendentals=0),
        compiler_params=params(16),
        name="near_sums",
    )(leg_t, a_own)


def piece_kernel(parts_ref, out_ref):
    piece = jnp.sum(parts_ref[...], axis=0)
    for i in range(out_ref.shape[0]):
        out_ref[i] = piece


def piece_copies(parts, copies):
    return pl.pallas_call(
        piece_kernel,
        in_specs=[VMEM],
        out_specs=VMEM,
        out_shape=jax.ShapeDtypeStruct((copies,) + parts.shape[1:], F32),
        compiler_params=params(8),
        name="piece_copies",
    )(parts)


def sketch_kernel(own_ref, other_ref, near_high_ref, near_low_ref, next_ref, high_ref, low_ref, sums_ref, sketch, high_buf, low_buf, sems):
    groups, own = own_ref.shape[1], own_ref.shape[3]
    columns, bond, quarter = near_high_ref.shape
    pairs = sketch.shape[1]
    width = 2 * pairs
    wide = own * bond
    parity = lax.axis_index("cols") % 2
    lane = iota((LANES, wide), 1) % bond
    keep = [(iota((LANES, wide), 0) == lane + half * bond).astype(BF16) for half in range(2)]
    same = iota((pairs * own, wide), 1) // bond == iota((pairs * own, wide), 0) % own

    def group(far_ref, odd, g, carry):
        far = far_ref[:, g].reshape(-1, LANES)[:pairs * own]
        parts = []
        for piece in halves(far):
            spread = [jnp.dot(piece, keep[half], preferred_element_type=F32) for half in range(2)]
            parts.append(jnp.concatenate([jnp.where(same, s, 0.0).astype(BF16) for s in spread], axis=0))
        first = pl.multiple_of((2 * g + odd) * own, own)
        near_high = near_high_ref[pl.ds(first, own)].reshape(wide, quarter)
        near_low = near_low_ref[pl.ds(first, own)].reshape(wide, quarter)
        left = jnp.concatenate([parts[0], parts[1], parts[0]], axis=1)
        right = jnp.concatenate([near_high, near_high, near_low], axis=0)
        result = jnp.dot(left, right, preferred_element_type=F32)
        sketch[:, :, pl.ds(first, own), :] = result.reshape(2, pairs, own, quarter)
        return carry

    lax.fori_loop(0, groups, functools.partial(group, own_ref, parity), 0)
    lax.fori_loop(0, groups, functools.partial(group, other_ref, 1 - parity), 0)

    def store(i, which):
        source, target = ((high_buf, high_ref), (low_buf, low_ref))[which]
        part = pl.ds(pl.multiple_of(8 * i, 8), 8)
        return pltpu.make_async_copy(source.at[part], target.at[part], sems.at[which, i])

    def products(i, total):
        for step in range(4):
            for half in range(2):
                y = 8 * i + 2 * step + half
                high, low = halves(sketch[half, 4 * i + step])
                high_buf[y] = high
                low_buf[y] = low
                both = jnp.concatenate([high, low], axis=0)
                left = jnp.concatenate([both, next_ref[y]], axis=0)
                total = total + lax.dot_general(left, both, NT, preferred_element_type=F32)
        store(i, 0).start()
        store(i, 1).start()
        return total

    rows = 2 * columns + bond
    total = lax.fori_loop(0, width // 8, products, jnp.zeros((rows, 2 * columns), F32))
    square = jnp.zeros((LANES, LANES), F32)
    padded = jnp.concatenate([jnp.concatenate([total, jnp.zeros((rows, LANES - 2 * columns), F32)], axis=1), square[rows:]], axis=0)
    turned = padded.T
    summed = turned[:columns] + turned[columns:2 * columns]
    gram = summed[:, :columns] + summed[:, columns:2 * columns]
    squeeze = summed[:, 2 * columns:rows]
    flat = jnp.concatenate([v[8 * i:8 * i + 8] for v in (gram, squeeze) for i in range(columns // 8)], axis=1)
    blocks = fold(flat)
    for copy in range(sums_ref.shape[0]):
        for i, block in enumerate(blocks):
            sums_ref[copy, i] = block
    for i in range(width // 8):
        store(i, 0).wait()
        store(i, 1).wait()


def fold(flat):
    blocks = []
    whole = flat.shape[1] // LANES * LANES
    for i in range(0, whole, LANES):
        blocks += [flat[:4, i:i + LANES], flat[4:, i:i + LANES]]
    if whole < flat.shape[1]:
        blocks.append(jnp.concatenate([flat[:4, whole:], flat[4:, whole:]], axis=1))
    return blocks


def unfold(blocks):
    flat = [jnp.concatenate(blocks[i:i + 2], axis=0) for i in range(0, len(blocks) - 1, 2)]
    if len(blocks) % 2:
        last = blocks[-1]
        flat.append(jnp.concatenate([last[:, :LANES // 2], last[:, LANES // 2:]], axis=0))
    return jnp.concatenate(flat, axis=1)


def sketch_products(far_own, far_other, near_high, near_low, nxt, copies):
    columns, bond, quarter = near_high.shape
    width = nxt.shape[0]
    shape = jax.ShapeDtypeStruct((width, columns, quarter), BF16)
    blocks = columns * (columns + bond) // 512
    held = pltpu.VMEM((width, columns, quarter), BF16)
    return pl.pallas_call(
        sketch_kernel,
        in_specs=[VMEM] * 5,
        out_specs=[HBM, HBM, VMEM],
        out_shape=[shape, shape, jax.ShapeDtypeStruct((copies, blocks, 4, LANES), F32)],
        scratch_shapes=[pltpu.VMEM((2, width // 2, columns, quarter), F32), held, held, pltpu.SemaphoreType.DMA((2, width // 8))],
        cost_estimate=pl.CostEstimate(flops=2 * columns * bond * width * quarter * 24, bytes_accessed=8 * columns * width * quarter, transcendentals=0),
        compiler_params=params(16),
        name="sketch_products",
    )(far_own, far_other, near_high, near_low, nxt)


def basis_kernel(count, sums_ref, high_ref, low_ref, basis_ref, squeezed_ref, square, high_buf, low_buf, out, in_sems, out_sems):
    width, columns, quarter = high_ref.shape
    bond = squeezed_ref.shape[1]

    def fetch(g, which):
        source, target = ((high_ref, high_buf), (low_ref, low_buf))[which]
        part = pl.ds(pl.multiple_of(8 * g, 8), 8)
        return pltpu.make_async_copy(source.at[part], target.at[part], in_sems.at[which, g])

    def store(g):
        return pltpu.make_async_copy(out.at[g], basis_ref.at[:, pl.ds(pl.multiple_of(8 * g, 8), 8), :], out_sems.at[g])

    for g in range(width // 8):
        fetch(g, 0).start()
        fetch(g, 1).start()
    summed = jnp.sum(sums_ref[...], axis=0)
    flat = unfold([summed[i] for i in range(summed.shape[0])])
    square[...] = jnp.zeros_like(square)
    for i in range(columns // 8):
        square[8 * i:8 * i + 8, :columns] = flat[:, i * columns:(i + 1) * columns] / count
        first = columns * (columns // 8) + i * bond
        square[8 * i:8 * i + 8, columns:columns + bond] = flat[:, first:first + bond]
    matrix = square[...]
    wide = 8 * columns
    unit = (iota((columns, wide), 1) % columns == iota((columns, wide), 0)).astype(F32)
    row = iota((columns, LANES), 0)
    roots = jnp.zeros((columns, LANES), F32)
    block = 4
    for first in range(0, columns, block):
        cols = [jnp.broadcast_to(matrix[:, first + j:first + j + 1], (columns, LANES)) for j in range(block)]
        for j in range(block):
            k = first + j
            pivot = cols[j][k:k + 1]
            factor = jnp.where(row > k, cols[j] * (1.0 / pivot), 0.0)
            for i in range(j + 1, block):
                cols[i] = cols[i] - factor * cols[i][k:k + 1]
            matrix = matrix - factor * matrix[k:k + 1]
            unit = unit - jnp.concatenate([factor] * (wide // LANES), axis=1) * unit[k:k + 1]
            roots = jnp.where(row == k, 1.0 / jnp.sqrt(pivot), roots)
    squeezed_ref[...] = (matrix * roots)[:, columns:columns + bond] / count ** 0.5
    inverse = unit * jnp.concatenate([roots] * (wide // LANES), axis=1)
    spread = jnp.broadcast_to(inverse[:, None, :], (columns, 8, wide)).reshape(wide, wide)
    same = iota((wide, wide), 1) // columns == iota((wide, wide), 0) % 8
    left_high, left_low = halves(jnp.where(same, spread, 0.0))

    def group(g, carry):
        fetch(g, 0).wait()
        fetch(g, 1).wait()
        first = pl.multiple_of(8 * g, 8)
        high = high_buf[pl.ds(first, 8)].reshape(wide, quarter)
        low = low_buf[pl.ds(first, 8)].reshape(wide, quarter)
        result = jnp.dot(left_high, high, preferred_element_type=F32)
        result += jnp.dot(left_low, high, preferred_element_type=F32)
        result += jnp.dot(left_high, low, preferred_element_type=F32)
        out[g] = result.reshape(columns, 8, quarter)
        store(g).start()
        return carry

    lax.fori_loop(0, width // 8, group, 0)
    lax.fori_loop(0, width // 8, lambda g, carry: (store(g).wait(), carry)[1], 0)


def basis_of(sums, high, low, bond, count):
    width, columns, quarter = high.shape
    held = pltpu.VMEM((width, columns, quarter), BF16)
    return pl.pallas_call(
        functools.partial(basis_kernel, float(count)),
        in_specs=[VMEM, HBM, HBM],
        out_specs=[HBM, VMEM],
        out_shape=[jax.ShapeDtypeStruct((columns, width, quarter), F32), jax.ShapeDtypeStruct((columns, bond), F32)],
        scratch_shapes=[
            pltpu.VMEM((columns, LANES), F32),
            held,
            held,
            pltpu.VMEM((width // 8, columns, 8, quarter), F32),
            pltpu.SemaphoreType.DMA((2, width // 8)),
            pltpu.SemaphoreType.DMA((width // 8,)),
        ],
        cost_estimate=pl.CostEstimate(flops=2 * columns * columns * width * quarter * 24, bytes_accessed=4 * columns * width * quarter, transcendentals=0),
        compiler_params=params(16),
        name="basis_of",
    )(sums, high, low)


def per_device(factor_a, factor_b, next_factor, sketch_leg, sketch_rows):
    rows, cols = lax.axis_size("rows"), lax.axis_size("cols")
    devices = rows * cols
    local_rows, width, bond = factor_a.shape
    quarter = local_rows // cols
    count = local_rows * rows * width
    a = jnp.transpose(factor_a, (1, 2, 0))
    b = jnp.transpose(factor_b, (1, 2, 0)).reshape(width // 2, 2 * bond, local_rows)
    nxt = jnp.transpose(next_factor, (1, 2, 0))
    own = sketch_rows.shape[1]
    b, a = (pltpu.with_memory_space_constraint(v, pltpu.HBM) for v in (b, a))
    partial, a_own = far_sum(sketch_rows.T, b, a, quarter)
    each = -(-(width // 2) // rows)
    partial = jnp.pad(partial, ((0, each * rows - width // 2), (0, 0), (0, 0))).reshape(rows, each, own, LANES)
    parts = lax.all_to_all(partial, "rows", 0, 0)
    parities = [[i for i in range(devices) if i % 2 == parity] for parity in range(2)]
    pieces = lax.all_to_all(piece_copies(parts, devices // 2), BOTH, 0, 0, axis_index_groups=parities)
    far_own = pieces.reshape(rows, cols // 2, each, own, LANES)
    far_other = lax.ppermute(far_own, "cols", [(i, i ^ 1) for i in range(cols)])
    near_high, near_low = near_sums(sketch_leg.T, a_own)
    high, low, sums = sketch_products(far_own, far_other, near_high, near_low, nxt, devices)
    basis, squeezed = basis_of(lax.all_to_all(sums, BOTH, 0, 0), high, low, bond, count)
    return jnp.transpose(basis, (0, 2, 1)), squeezed


def solution(mesh):
    return jax.shard_map(
        per_device,
        mesh=mesh,
        in_specs=(
            P("rows", None, None),
            P("rows", None, None),
            P(BOTH, None, None),
            P(),
            P("rows", "cols"),
        ),
        out_specs=(P(None, BOTH, None), P()),
        check_vma=False,
    )
```

time: 90.5 us -> 59.9 us (0.66)
  matrix products: 33.1 us -> 0 us
  Pallas kernels: 0 us -> 18.5 us
  blocking collectives: 29.7 us -> 39.7 us
  waiting for transfers between devices: 8 us -> 0.01 us
  local copies, waits for them, and re-layouts: 8.35 us -> 0.76 us
  other arithmetic: 6.82 us -> 0 us
  starting transfers between devices: 3.3 us -> 0.01 us
    dot_general x7 -> x0, matrix products: 32.9 us -> none  [the longest x1 7.16 us: per_device(): jnp.einsum('sp,yks->pyk', sketch_rows, b, preferred_element_type=f32)]
    pallas_call x0 -> x5, Pallas kernels: none -> 18.5 us  [the longest x1 6.3 us: sketch_products(): pl.pallas_call(sketch_kernel, in_specs=[VMEM] * 5, out_specs=[HBM, HBM, V...]
    all_to_all x2 -> x3, blocking collectives: 29.7 us -> 39.7 us  [the longest x1 14.2 us: per_device(): parts = lax.all_to_all(partial, 'rows', 0, 0)]
    all_to_all x1 -> x0, waiting for transfers between devices: 8 us -> none  [gather_all(): lax.all_to_all(jnp.broadcast_to(value[None], (parts,) + value.shape), BOT...]
    another operation x5 -> x0, other arithmetic: 6.68 us -> none  [the longest x3 3.59 us: per_device(): lower = jnp.linalg.cholesky(gram)]
    all_to_all x1 -> x0, starting transfers between devices: 3.3 us -> none  [gather_all(): lax.all_to_all(jnp.broadcast_to(value[None], (parts,) + value.shape), BOT...]
    unnamed x8 -> x6, local copies, waits for them, and re-layouts: 3.59 us -> 0.76 us
    reshape x4 -> x0, local copies, waits for them, and re-layouts: 1.85 us -> none  [the longest x1 1.57 us: per_device(): far = gather_all(piece).reshape(rows, cols * own, each, bond)]
  transfers between devices with their start and end apart: 1 -> 1, of which waited for: 1 -> 0; matrix products, arithmetic and copies ran while one was open for 6% -> 0% of each run, Pallas kernels for 0% -> 3%
where the time goes in v2:
time: 59.9 us; the launch traced here: 59.6 us
  blocking collectives  39.7 us (66%)
  Pallas kernels  18.5 us (31%)
  local copies, waits for them, and re-layouts  0.76 us (1%)
  between operations  0.69 us (1%)
    all_to_all x1, blocking collectives, per_device(): parts = lax.all_to_all(partial, 'rows', 0, 0)  14.2 us
    all_to_all x1, blocking collectives, per_device(): lax.all_to_all(sums, BOTH, 0, 0)  14.2 us
    all_to_all x1, blocking collectives, per_device(): lax.all_to_all(piece_copies(parts, devices // 2), BOTH, 0, 0, axis_index_...  11.3 us
    pallas_call x1, Pallas kernels, sketch_products(): pl.pallas_call(sketch_kernel, in_specs=[VMEM] * 5, out_specs=[HBM, HBM, V...  6.3 us
    pallas_call x1, Pallas kernels, basis_of(): pl.pallas_call(functools.partial(basis_kernel, float(count)), in_specs=[V...  5.51 us
    pallas_call x1, Pallas kernels, far_sum(): pl.pallas_call(far_kernel, in_specs=[VMEM, HBM, HBM], out_specs=[VMEM, VM...  5.12 us
    pallas_call x1, Pallas kernels, near_sums(): pl.pallas_call(near_kernel, in_specs=[VMEM, VMEM], out_specs=[VMEM, VMEM]...  1.51 us
  transfers between devices with their start and end apart: 1, of which 0 were waited for; matrix products, arithmetic and copies ran while one was open for 0% of the time, Pallas kernels for 3%

profile of v2, /device:TPU:0, one launch (start us, length us, event | category | flops | bytes accessed | tf_op | source)
XLA Modules:
  0.0 59.6 jit_solution(2210622278570940469)
XLA Ops:
  0.6 0.0 copy-start
  0.6 0.7 %copy-done = bf16[2048,8]{0,1:T(8,128)(2,1)S(1)} copy-done((bf16[2048,8]{0,1:T(8,128)(2,1)S(1)}, bf16[2048,8]{0,1:T(8,128)(2,1)}, u32[]{:S(2)}) %copy-start) | copy-done | bytes 32792
  1.4 0.0 copy-start.2
  1.4 5.1 %far_sum.1 = (f32[24,8,128]{2,1,0:T(8,128)S(1)}, bf16[48,48,512]{2,1,0:T(8,128)(2,1)S(1)}) custom-call(bf16[8,2048]{1,0:T(8,128)(2,1)S(1)} %bitcast.13, bf16[24,96,2048]{2,1,0:T(8,128)(2,1)} %bitcast.16, bf16[48,48,2048]{2,1,0:T(8,128)(2,1)} %bitcast.17), custom_call_target="tpu_custom_call" | custom-call | flops 75497472 | bytes 9437184 | tf_op jit(solution)/shard_map/far_sum/pallas_call | solution.py:60
  6.5 14.2 %all_to_all.15.parts_ref = f32[8,3,8,128]{3,2,1,0:T(8,128)S(1)} all-to-all(f32[8,3,8,128]{3,2,1,0:T(8,128)S(1)} %bitcast.12), channel_id=1, replica_groups=mesh['rows'=8,'cols'=4] {'rows'}, dimensions={0} | all-to-all | bytes 196608 | tf_op jit(solution)/shard_map/all_to_all | solution.py:321
  20.8 0.0 copy-start.1
  20.8 11.3 %all_to_all.16 = f32[16,3,8,128]{3,2,1,0:T(8,128)S(1)} all-to-all(f32[16,3,8,128]{3,2,1,0:T(8,128)S(1)} %piece_copies.1), channel_id=1, replica_groups={{0,2,4,6,8,10,12,14,16,18,20,22,24,26,28,30},{1,3,5,7,9,11,13,15,17,19,..., dimensions={0} | all-to-all | bytes 393216 | tf_op jit(solution)/shard_map/all_to_all | solution.py:323
  32.1 0.0 collective-permute-start
  32.1 0.0 copy-done.2
  32.1 1.5 %near_sums.1 = (bf16[32,48,512]{2,1,0:T(8,128)(2,1)S(1)}, bf16[32,48,512]{2,1,0:T(8,128)(2,1)S(1)}) custom-call(bf16[32,48]{1,0:T(8,128)(2,1)S(1)} %bitcast.15, bf16[48,48,512]{2,1,0:T(8,128)(2,1)S(1)} %get-tuple-element.12.a_ref), custom_call_target="tpu_custom_call" | custom-call | flops 1207959552 | bytes 2359296 | tf_op jit(solution)/shard_map/near_sums/pallas_call | solution.py:93
  33.6 0.0 collective-permute-done.other_ref
  33.6 0.0 copy-done.1
  33.6 6.3 %sketch_products.1 = (bf16[48,32,512]{2,1,0:T(8,128)(2,1)S(1)}, bf16[48,32,512]{2,1,0:T(8,128)(2,1)S(1)}, f32[32,5,4,128]{3,2,1,0:T(4,128)S(1)}) custom-call(f32[8,2,3,8,128]{4,3,2,1,0:T(8,128)S(1)} %bitcast.11, f32[8,2,3,8,128]{4,3,2,1,0:T(8,128)S(1)} %collective-permute-done.other_ref, bf16[32,48,512]{2,1,0:T(8,128)(2,1)S(1)} %get-tuple-element.13.near_high_ref, ...), custom_call_target="tpu_custom_call" | custom-call | flops 1811939328 | bytes 6291456 | tf_op jit(solution)/shard_map/sketch_products/pallas_call | solution.py:211
  39.9 14.2 %all_to_all.17.sums_ref = f32[32,5,4,128]{3,2,1,0:T(4,128)S(1)} all-to-all(f32[32,5,4,128]{3,2,1,0:T(4,128)S(1)} %get-tuple-element.15), channel_id=1, replica_groups=mesh['rows'=8,'cols'=4] {'rows','cols'}, dimensions={0} | all-to-all | bytes 655360 | tf_op jit(solution)/shard_map/all_to_all | solution.py:328
  54.1 5.5 %basis_of.1 = (f32[32,48,512]{2,1,0:T(8,128)}, f32[32,48]{1,0:T(8,128)}) custom-call(f32[32,5,4,128]{3,2,1,0:T(4,128)S(1)} %all_to_all.17.sums_ref, bf16[48,32,512]{2,1,0:T(8,128)(2,1)S(1)} %get-tuple-element.16.high_ref, bf16[48,32,512]{2,1,0:T(8,128)(2,1)S(1)} %get-tuple-element.17.low_ref), custom_call_target="tpu_custom_call" | custom-call | flops 1207959552 | bytes 3145728 | tf_op jit(solution)/shard_map/basis_of/pallas_call | solution.py:288
  (1 shorter events, 0.0 us)
Async XLA Ops:
  0.6 0.8 %copy-start = (bf16[2048,8]{0,1:T(8,128)(2,1)S(1)}, bf16[2048,8]{0,1:T(8,128)(2,1)}, u32[]{:S(2)}) copy-start(bf16[2048,8]{0,1:T(8,128)(2,1)} %param.9) | copy-start | bytes 98308
  1.4 30.7 %copy-start.2 = (bf16[48,32]{0,1:T(8,128)(2,1)S(1)}, bf16[48,32]{0,1:T(8,128)(2,1)}, u32[]{:S(2)}) copy-start(bf16[48,32]{0,1:T(8,128)(2,1)} %param.8) | copy-start | bytes 9220
  20.8 12.8 %copy-start.1 = (bf16[512,48,48]{0,2,1:T(8,128)(2,1)S(1)}, bf16[512,48,48]{0,2,1:T(8,128)(2,1)}, u32[]{:S(2)}) copy-start(bf16[512,48,48]{0,2,1:T(8,128)(2,1)} %param.7) | copy-start | bytes 7077892
  32.1 1.5 %collective-permute-start = (f32[8,2,3,8,128]{4,3,2,1,0:T(8,128)S(1)}, f32[8,2,3,8,128]{4,3,2,1,0:T(8,128)S(1)}, u32[]{:S(2)}, u32[]{:S(2)}) collective-permute-start(f32[8,2,3,8,128]{4,3,2,1,0:T(8,128)S(1)} %bitcast.10), channel_id=1, source_target_pairs={{0,1},{1,0},{2,3},{3,2},{4,5},{5,4},{6,7},{7,6},{8,9},{9,8},{10,11... | collective-permute-start | bytes 589832 | tf_op jit(solution)/shard_map/ppermute | solution.py:325

commit v3 on v2

--- a/solution.py
+++ b/solution.py
@@ -28,7 +28,7 @@
     return pltpu.CompilerParams(vmem_limit_bytes=mib << 20)
 
 
-def far_kernel(rows_ref, b_ref, a_ref, out_ref, own_ref, buf, sems, own_sem):
+def far_kernel(rows_ref, b_ref, a_ref, out_ref, own_ref, rows_buf, buf, rows_sem, own_sem, sems):
     pairs, used, _ = b_ref.shape
     chunks = sems.shape[0]
     step = pairs // chunks
@@ -39,30 +39,42 @@
         part = pl.ds(c * step, step)
         return pltpu.make_async_copy(b_ref.at[part], buf.at[part], sems.at[c])
 
-    for c in range(chunks):
+    rows_copy = pltpu.make_async_copy(rows_ref, rows_buf, rows_sem)
+    rows_copy.start()
+    ahead = 2
+    for c in range(ahead):
         fetch(c).start()
     own_copy = pltpu.make_async_copy(a_ref.at[:, :, pl.ds(start, quarter)], own_ref, own_sem)
-    own_copy.start()
     own, lanes = out_ref.shape[1:]
     out_ref[:, :, used:] = jnp.zeros((pairs, own, lanes - used), F32)
+    rows_copy.wait()
+    for c in range(ahead, chunks):
+        fetch(c).start()
+    own_copy.start()
     for c in range(chunks):
         fetch(c).wait()
         for i in range(step):
             pair = c * step + i
-            out_ref[pair, :, :used] = lax.dot_general(rows_ref[...], buf[pair], NT, preferred_element_type=F32)
+            out_ref[pair, :, :used] = lax.dot_general(rows_buf[...], buf[pair], NT, preferred_element_type=F32)
     own_copy.wait()
 
 
 def far_sum(rows_t, b_pairs, a_t, quarter):
     pairs, used, depth = b_pairs.shape
-    chunks = pairs // 2
+    chunks = pairs // 6
     own = rows_t.shape[0]
     return pl.pallas_call(
         far_kernel,
-        in_specs=[VMEM, HBM, HBM],
-        out_specs=[VMEM, VMEM],
+        in_specs=[HBM] * 3,
+        out_specs=[VMEM] * 2,
         out_shape=[jax.ShapeDtypeStruct((pairs, own, LANES), F32), jax.ShapeDtypeStruct(a_t.shape[:2] + (quarter,), BF16)],
-        scratch_shapes=[pltpu.VMEM((pairs, used, depth), BF16), pltpu.SemaphoreType.DMA((chunks,)), pltpu.SemaphoreType.DMA],
+        scratch_shapes=[
+            pltpu.VMEM(rows_t.shape, BF16),
+            pltpu.VMEM((pairs, used, depth), BF16),
+            pltpu.SemaphoreType.DMA,
+            pltpu.SemaphoreType.DMA,
+            pltpu.SemaphoreType.DMA((chunks,)),
+        ],
         cost_estimate=pl.CostEstimate(flops=2 * own * pairs * used * depth, bytes_accessed=2 * pairs * used * depth, transcendentals=0),
         compiler_params=params(16),
         name="far_sum",
@@ -71,7 +83,7 @@
 
 def near_kernel(leg_ref, a_ref, high_ref, low_ref):
     columns, width = leg_ref.shape
-    _, bond, quarter = a_ref.shape
+    _, bond, quarter = high_ref.shape
     deep = 16
     wide = width * deep
     spread = (iota((width, wide), 1) // deep == iota((width, wide), 0)).astype(BF16)
@@ -118,7 +130,7 @@
     )(parts)
 
 
-def sketch_kernel(own_ref, other_ref, near_high_ref, near_low_ref, next_ref, high_ref, low_ref, sums_ref, sketch, high_buf, low_buf, sems):
+def sketch_kernel(own_ref, other_ref, near_high_ref, near_low_ref, next_ref, high_ref, low_ref, sums_ref, sketch):
     groups, own = own_ref.shape[1], own_ref.shape[3]
     columns, bond, quarter = near_high_ref.shape
     pairs = sketch.shape[1]
@@ -147,23 +159,16 @@
     lax.fori_loop(0, groups, functools.partial(group, own_ref, parity), 0)
     lax.fori_loop(0, groups, functools.partial(group, other_ref, 1 - parity), 0)
 
-    def store(i, which):
-        source, target = ((high_buf, high_ref), (low_buf, low_ref))[which]
-        part = pl.ds(pl.multiple_of(8 * i, 8), 8)
-        return pltpu.make_async_copy(source.at[part], target.at[part], sems.at[which, i])
-
     def products(i, total):
         for step in range(4):
             for half in range(2):
                 y = 8 * i + 2 * step + half
                 high, low = halves(sketch[half, 4 * i + step])
-                high_buf[y] = high
-                low_buf[y] = low
+                high_ref[y] = high
+                low_ref[y] = low
                 both = jnp.concatenate([high, low], axis=0)
                 left = jnp.concatenate([both, next_ref[y]], axis=0)
                 total = total + lax.dot_general(left, both, NT, preferred_element_type=F32)
-        store(i, 0).start()
-        store(i, 1).start()
         return total
 
     rows = 2 * columns + bond
@@ -179,9 +184,6 @@
     for copy in range(sums_ref.shape[0]):
         for i, block in enumerate(blocks):
             sums_ref[copy, i] = block
-    for i in range(width // 8):
-        store(i, 0).wait()
-        store(i, 1).wait()
 
 
 def fold(flat):
@@ -207,34 +209,25 @@
     width = nxt.shape[0]
     shape = jax.ShapeDtypeStruct((width, columns, quarter), BF16)
     blocks = columns * (columns + bond) // 512
-    held = pltpu.VMEM((width, columns, quarter), BF16)
     return pl.pallas_call(
         sketch_kernel,
         in_specs=[VMEM] * 5,
-        out_specs=[HBM, HBM, VMEM],
+        out_specs=[VMEM] * 3,
         out_shape=[shape, shape, jax.ShapeDtypeStruct((copies, blocks, 4, LANES), F32)],
-        scratch_shapes=[pltpu.VMEM((2, width // 2, columns, quarter), F32), held, held, pltpu.SemaphoreType.DMA((2, width // 8))],
+        scratch_shapes=[pltpu.VMEM((2, width // 2, columns, quarter), F32)],
         cost_estimate=pl.CostEstimate(flops=2 * columns * bond * width * quarter * 24, bytes_accessed=8 * columns * width * quarter, transcendentals=0),
         compiler_params=params(16),
         name="sketch_products",
     )(far_own, far_other, near_high, near_low, nxt)
 
 
-def basis_kernel(count, sums_ref, high_ref, low_ref, basis_ref, squeezed_ref, square, high_buf, low_buf, out, in_sems, out_sems):
+def basis_kernel(count, sums_ref, high_ref, low_ref, basis_ref, squeezed_ref, square, out, out_sems):
     width, columns, quarter = high_ref.shape
     bond = squeezed_ref.shape[1]
 
-    def fetch(g, which):
-        source, target = ((high_ref, high_buf), (low_ref, low_buf))[which]
-        part = pl.ds(pl.multiple_of(8 * g, 8), 8)
-        return pltpu.make_async_copy(source.at[part], target.at[part], in_sems.at[which, g])
-
     def store(g):
         return pltpu.make_async_copy(out.at[g], basis_ref.at[:, pl.ds(pl.multiple_of(8 * g, 8), 8), :], out_sems.at[g])
 
-    for g in range(width // 8):
-        fetch(g, 0).start()
-        fetch(g, 1).start()
     summed = jnp.sum(sums_ref[...], axis=0)
     flat = unfold([summed[i] for i in range(summed.shape[0])])
     square[...] = jnp.zeros_like(square)
@@ -266,11 +259,9 @@
     left_high, left_low = halves(jnp.where(same, spread, 0.0))
 
     def group(g, carry):
-        fetch(g, 0).wait()
-        fetch(g, 1).wait()
         first = pl.multiple_of(8 * g, 8)
-        high = high_buf[pl.ds(first, 8)].reshape(wide, quarter)
-        low = low_buf[pl.ds(first, 8)].reshape(wide, quarter)
+        high = high_ref[pl.ds(first, 8)].reshape(wide, quarter)
+        low = low_ref[pl.ds(first, 8)].reshape(wide, quarter)
         result = jnp.dot(left_high, high, preferred_element_type=F32)
         result += jnp.dot(left_low, high, preferred_element_type=F32)
         result += jnp.dot(left_high, low, preferred_element_type=F32)
@@ -284,18 +275,14 @@
 
 def basis_of(sums, high, low, bond, count):
     width, columns, quarter = high.shape
-    held = pltpu.VMEM((width, columns, quarter), BF16)
     return pl.pallas_call(
         functools.partial(basis_kernel, float(count)),
-        in_specs=[VMEM, HBM, HBM],
+        in_specs=[VMEM] * 3,
         out_specs=[HBM, VMEM],
         out_shape=[jax.ShapeDtypeStruct((columns, width, quarter), F32), jax.ShapeDtypeStruct((columns, bond), F32)],
         scratch_shapes=[
             pltpu.VMEM((columns, LANES), F32),
-            held,
-            held,
             pltpu.VMEM((width // 8, columns, 8, quarter), F32),
-            pltpu.SemaphoreType.DMA((2, width // 8)),
             pltpu.SemaphoreType.DMA((width // 8,)),
         ],
         cost_estimate=pl.CostEstimate(flops=2 * columns * columns * width * quarter * 24, bytes_accessed=4 * columns * width * quarter, transcendentals=0),
@@ -314,8 +301,8 @@
     b = jnp.transpose(factor_b, (1, 2, 0)).reshape(width // 2, 2 * bond, local_rows)
     nxt = jnp.transpose(next_factor, (1, 2, 0))
     own = sketch_rows.shape[1]
-    b, a = (pltpu.with_memory_space_constraint(v, pltpu.HBM) for v in (b, a))
-    partial, a_own = far_sum(sketch_rows.T, b, a, quarter)
+    operands = [pltpu.with_memory_space_constraint(v, pltpu.HBM) for v in (sketch_rows.T, b, a)]
+    partial, a_own = far_sum(*operands, quarter)
     each = -(-(width // 2) // rows)
     partial = jnp.pad(partial, ((0, each * rows - width // 2), (0, 0), (0, 0))).reshape(rows, each, own, LANES)
     parts = lax.all_to_all(partial, "rows", 0, 0)

time: 59.9 us -> 58.1 us (0.970)
  Pallas kernels: 18.5 us -> 17.5 us
  local copies, waits for them, and re-layouts: 0.76 us -> 0.01 us
    unnamed x6 -> x4, local copies, waits for them, and re-layouts: 0.76 us -> 0.01 us
where the time goes in v3:
time: 58.1 us; the launch traced here: 57.9 us
  blocking collectives  39.7 us (68%)
  Pallas kernels  17.5 us (30%)
  between operations  0.69 us (1%)
    all_to_all x1, blocking collectives, per_device(): parts = lax.all_to_all(partial, 'rows', 0, 0)  14.2 us
    all_to_all x1, blocking collectives, per_device(): lax.all_to_all(sums, BOTH, 0, 0)  14.2 us
    all_to_all x1, blocking collectives, per_device(): lax.all_to_all(piece_copies(parts, devices // 2), BOTH, 0, 0, axis_index_...  11.3 us
    pallas_call x1, Pallas kernels, sketch_products(): pl.pallas_call(sketch_kernel, in_specs=[VMEM] * 5, out_specs=[VMEM] * 3,...  5.95 us
    pallas_call x1, Pallas kernels, basis_of(): pl.pallas_call(functools.partial(basis_kernel, float(count)), in_specs=[V...  5.15 us
    pallas_call x1, Pallas kernels, far_sum(): pl.pallas_call(far_kernel, in_specs=[HBM] * 3, out_specs=[VMEM] * 2, out_...  4.9 us
    pallas_call x1, Pallas kernels, near_sums(): pl.pallas_call(near_kernel, in_specs=[VMEM, VMEM], out_specs=[VMEM, VMEM]...  1.52 us
  transfers between devices with their start and end apart: 1, of which 0 were waited for; matrix products, arithmetic and copies ran while one was open for 0% of the time, Pallas kernels for 3%

profile of v3, /device:TPU:0, one launch (start us, length us, event | category | flops | bytes accessed | tf_op | source)
XLA Modules:
  0.0 57.9 jit_solution(5889367265914863562)
XLA Ops:
  0.6 0.0 copy-start.1
  0.6 4.9 %far_sum.1 = (f32[24,8,128]{2,1,0:T(8,128)S(1)}, bf16[48,48,512]{2,1,0:T(8,128)(2,1)S(1)}) custom-call(bf16[8,2048]{1,0:T(8,128)(2,1)} %bitcast.17, bf16[24,96,2048]{2,1,0:T(8,128)(2,1)} %bitcast.15, bf16[48,48,2048]{2,1,0:T(8,128)(2,1)} %bitcast.16), custom_call_target="tpu_custom_call" | custom-call | flops 75497472 | bytes 9437184 | tf_op jit(solution)/shard_map/far_sum/pallas_call | solution.py:66
  5.5 14.2 %all_to_all.15.parts_ref = f32[8,3,8,128]{3,2,1,0:T(8,128)S(1)} all-to-all(f32[8,3,8,128]{3,2,1,0:T(8,128)S(1)} %bitcast.12), channel_id=1, replica_groups=mesh['rows'=8,'cols'=4] {'rows'}, dimensions={0} | all-to-all | bytes 196608 | tf_op jit(solution)/shard_map/all_to_all | solution.py:308
  19.8 0.0 copy-start
  19.8 11.3 %all_to_all.16 = f32[16,3,8,128]{3,2,1,0:T(8,128)S(1)} all-to-all(f32[16,3,8,128]{3,2,1,0:T(8,128)S(1)} %piece_copies.1), channel_id=1, replica_groups={{0,2,4,6,8,10,12,14,16,18,20,22,24,26,28,30},{1,3,5,7,9,11,13,15,17,19,..., dimensions={0} | all-to-all | bytes 393216 | tf_op jit(solution)/shard_map/all_to_all | solution.py:310
  31.1 0.0 collective-permute-start
  31.1 0.0 copy-done.1
  31.1 1.5 %near_sums.1 = (bf16[32,48,512]{2,1,0:T(8,128)(2,1)S(1)}, bf16[32,48,512]{2,1,0:T(8,128)(2,1)S(1)}) custom-call(bf16[32,48]{1,0:T(8,128)(2,1)S(1)} %bitcast.14, bf16[48,48,512]{2,1,0:T(8,128)(2,1)S(1)} %get-tuple-element.12.a_ref), custom_call_target="tpu_custom_call" | custom-call | flops 1207959552 | bytes 2359296 | tf_op jit(solution)/shard_map/near_sums/pallas_call | solution.py:105
  32.6 0.0 collective-permute-done.other_ref
  32.6 0.0 copy-done
  32.6 5.9 %sketch_products.1 = (bf16[48,32,512]{2,1,0:T(8,128)(2,1)S(1)}, bf16[48,32,512]{2,1,0:T(8,128)(2,1)S(1)}, f32[32,5,4,128]{3,2,1,0:T(4,128)S(1)}) custom-call(f32[8,2,3,8,128]{4,3,2,1,0:T(8,128)S(1)} %bitcast.11, f32[8,2,3,8,128]{4,3,2,1,0:T(8,128)S(1)} %collective-permute-done.other_ref, bf16[32,48,512]{2,1,0:T(8,128)(2,1)S(1)} %get-tuple-element.13.near_high_ref, ...), custom_call_target="tpu_custom_call" | custom-call | flops 1811939328 | bytes 6291456 | tf_op jit(solution)/shard_map/sketch_products/pallas_call | solution.py:212
  38.6 14.2 %all_to_all.17.sums_ref = f32[32,5,4,128]{3,2,1,0:T(4,128)S(1)} all-to-all(f32[32,5,4,128]{3,2,1,0:T(4,128)S(1)} %get-tuple-element.15), channel_id=1, replica_groups=mesh['rows'=8,'cols'=4] {'rows','cols'}, dimensions={0} | all-to-all | bytes 655360 | tf_op jit(solution)/shard_map/all_to_all | solution.py:315
  52.8 5.1 %basis_of.1 = (f32[32,48,512]{2,1,0:T(8,128)}, f32[32,48]{1,0:T(8,128)}) custom-call(f32[32,5,4,128]{3,2,1,0:T(4,128)S(1)} %all_to_all.17.sums_ref, bf16[48,32,512]{2,1,0:T(8,128)(2,1)S(1)} %get-tuple-element.16.high_ref, bf16[48,32,512]{2,1,0:T(8,128)(2,1)S(1)} %get-tuple-element.17.low_ref), custom_call_target="tpu_custom_call" | custom-call | flops 1207959552 | bytes 3145728 | tf_op jit(solution)/shard_map/basis_of/pallas_call | solution.py:278
  (1 shorter events, 0.0 us)
Async XLA Ops:
  0.6 30.5 %copy-start.1 = (bf16[48,32]{0,1:T(8,128)(2,1)S(1)}, bf16[48,32]{0,1:T(8,128)(2,1)}, u32[]{:S(2)}) copy-start(bf16[48,32]{0,1:T(8,128)(2,1)} %param.8) | copy-start | bytes 9220
  19.8 12.8 %copy-start = (bf16[512,48,48]{0,2,1:T(8,128)(2,1)S(1)}, bf16[512,48,48]{0,2,1:T(8,128)(2,1)}, u32[]{:S(2)}) copy-start(bf16[512,48,48]{0,2,1:T(8,128)(2,1)} %param.7) | copy-start | bytes 7077892
  31.1 1.5 %collective-permute-start = (f32[8,2,3,8,128]{4,3,2,1,0:T(8,128)S(1)}, f32[8,2,3,8,128]{4,3,2,1,0:T(8,128)S(1)}, u32[]{:S(2)}, u32[]{:S(2)}) collective-permute-start(f32[8,2,3,8,128]{4,3,2,1,0:T(8,128)S(1)} %bitcast.10), channel_id=1, source_target_pairs={{0,1},{1,0},{2,3},{3,2},{4,5},{5,4},{6,7},{7,6},{8,9},{9,8},{10,11... | collective-permute-start | bytes 589832 | tf_op jit(solution)/shard_map/ppermute | solution.py:312

commit v4 on v3

--- a/solution.py
+++ b/solution.py
@@ -113,15 +113,21 @@
     )(leg_t, a_own)
 
 
-def piece_kernel(parts_ref, out_ref):
+def piece_kernel(bond, parts_ref, out_ref):
     piece = jnp.sum(parts_ref[...], axis=0)
+    half = piece.shape[1] // 2
+    crossed = pltpu.roll(piece, half, 1)
+    upper = iota(piece.shape, 1) < half
+    left = iota(piece.shape, 2) < bond
+    crossed = jnp.where(upper, pltpu.roll(crossed, bond, 2), pltpu.roll(crossed, LANES - bond, 2))
+    piece = jnp.where(upper == left, piece, crossed)
     for i in range(out_ref.shape[0]):
         out_ref[i] = piece
 
 
-def piece_copies(parts, copies):
-    return pl.pallas_call(
-        piece_kernel,
+def piece_copies(parts, copies, bond):
+    return pl.pallas_call(
+        functools.partial(piece_kernel, bond),
         in_specs=[VMEM],
         out_specs=VMEM,
         out_shape=jax.ShapeDtypeStruct((copies,) + parts.shape[1:], F32),
@@ -133,27 +139,25 @@
 def sketch_kernel(own_ref, other_ref, near_high_ref, near_low_ref, next_ref, high_ref, low_ref, sums_ref, sketch):
     groups, own = own_ref.shape[1], own_ref.shape[3]
     columns, bond, quarter = near_high_ref.shape
-    pairs = sketch.shape[1]
-    width = 2 * pairs
-    wide = own * bond
+    pairs = sketch.shape[0]
+    part = own // 2
+    wide = part * bond
     parity = lax.axis_index("cols") % 2
     lane = iota((LANES, wide), 1) % bond
     keep = [(iota((LANES, wide), 0) == lane + half * bond).astype(BF16) for half in range(2)]
-    same = iota((pairs * own, wide), 1) // bond == iota((pairs * own, wide), 0) % own
+    same = iota((pairs * own, wide), 1) // bond == iota((pairs * own, wide), 0) % part
 
     def group(far_ref, odd, g, carry):
-        far = far_ref[:, g].reshape(-1, LANES)[:pairs * own]
-        parts = []
-        for piece in halves(far):
-            spread = [jnp.dot(piece, keep[half], preferred_element_type=F32) for half in range(2)]
-            parts.append(jnp.concatenate([jnp.where(same, s, 0.0).astype(BF16) for s in spread], axis=0))
-        first = pl.multiple_of((2 * g + odd) * own, own)
-        near_high = near_high_ref[pl.ds(first, own)].reshape(wide, quarter)
-        near_low = near_low_ref[pl.ds(first, own)].reshape(wide, quarter)
-        left = jnp.concatenate([parts[0], parts[1], parts[0]], axis=1)
-        right = jnp.concatenate([near_high, near_high, near_low], axis=0)
-        result = jnp.dot(left, right, preferred_element_type=F32)
-        sketch[:, :, pl.ds(first, own), :] = result.reshape(2, pairs, own, quarter)
+        far = halves(far_ref[:, g].reshape(-1, LANES)[:pairs * own])
+        for half in range(2):
+            spread = [jnp.dot(piece, keep[half], preferred_element_type=F32) for piece in far]
+            high, low = (jnp.where(same, value, 0.0).astype(BF16) for value in spread)
+            block = 2 * (2 * g + odd) + half
+            near_high = near_high_ref[pl.ds(block * part, part)].reshape(wide, quarter)
+            near_low = near_low_ref[pl.ds(block * part, part)].reshape(wide, quarter)
+            both = jnp.dot(jnp.concatenate([high, low], axis=0), near_high, preferred_element_type=F32)
+            result = both[:pairs * own] + both[pairs * own:] + jnp.dot(high, near_low, preferred_element_type=F32)
+            sketch[:, pl.ds(pl.multiple_of(block * own, own), own), :] = result.reshape(pairs, own, quarter)
         return carry
 
     lax.fori_loop(0, groups, functools.partial(group, own_ref, parity), 0)
@@ -161,29 +165,38 @@
 
     def products(i, total):
         for step in range(4):
-            for half in range(2):
-                y = 8 * i + 2 * step + half
-                high, low = halves(sketch[half, 4 * i + step])
-                high_ref[y] = high
-                low_ref[y] = low
-                both = jnp.concatenate([high, low], axis=0)
-                left = jnp.concatenate([both, next_ref[y]], axis=0)
-                total = total + lax.dot_general(left, both, NT, preferred_element_type=F32)
+            pair = 4 * i + step
+            high, low = halves(sketch[pair])
+            high_ref[pair] = high
+            low_ref[pair] = low
+            left = jnp.concatenate([high, next_ref[2 * pair], next_ref[2 * pair + 1]], axis=0)
+            total = total + lax.dot_general(left, jnp.concatenate([high, low], axis=0), NT, preferred_element_type=F32)
         return total
 
-    rows = 2 * columns + bond
-    total = lax.fori_loop(0, width // 8, products, jnp.zeros((rows, 2 * columns), F32))
-    square = jnp.zeros((LANES, LANES), F32)
-    padded = jnp.concatenate([jnp.concatenate([total, jnp.zeros((rows, LANES - 2 * columns), F32)], axis=1), square[rows:]], axis=0)
+    doubled = 2 * columns
+    rows = doubled + 2 * bond
+    total = lax.fori_loop(0, pairs // 4, products, jnp.zeros((rows, LANES), F32))
+    row, lane = iota((rows, LANES), 0), iota((rows, LANES), 1)
+    row_y = jnp.where(row < doubled, row // part % 2, (row >= doubled + bond).astype(jnp.int32))
+    total = jnp.where(row_y == lane // part % 2, total, 0.0)
+    lane, target = iota((LANES, doubled), 0), iota((LANES, doubled), 1)
+    column = lane % doubled // own * part + lane % part
+    pick = (column == target % columns) & ((target < columns) | (lane >= doubled))
+    packed = jnp.dot(total, pick.astype(F32), preferred_element_type=F32, precision=lax.Precision.HIGHEST)
+    squares = packed[:doubled].reshape(doubled // own, own, doubled)
+    squares = squares + pltpu.roll(squares, part, 1)
+    upper = iota((own, doubled), 0) < part
+    squares = jnp.concatenate([jnp.where(upper, squares[2 * i], squares[2 * i + 1]) for i in range(columns // own)], axis=0)
+    squeezes = packed[doubled:doubled + bond] + packed[doubled + bond:]
+    padded = jnp.concatenate([squares, squeezes, jnp.zeros((LANES - columns - bond, doubled), F32)], axis=0)
+    padded = jnp.concatenate([padded, jnp.zeros((LANES, LANES - doubled), F32)], axis=1)
     turned = padded.T
-    summed = turned[:columns] + turned[columns:2 * columns]
-    gram = summed[:, :columns] + summed[:, columns:2 * columns]
-    squeeze = summed[:, 2 * columns:rows]
+    gram = squares[:, :columns] + turned[columns:doubled, :columns]
+    squeeze = turned[:columns, columns:columns + bond]
     flat = jnp.concatenate([v[8 * i:8 * i + 8] for v in (gram, squeeze) for i in range(columns // 8)], axis=1)
     blocks = fold(flat)
-    for copy in range(sums_ref.shape[0]):
-        for i, block in enumerate(blocks):
-            sums_ref[copy, i] = block
+    for i, block in enumerate(blocks):
+        sums_ref[i] = block
 
 
 def fold(flat):
@@ -204,25 +217,42 @@
     return jnp.concatenate(flat, axis=1)
 
 
-def sketch_products(far_own, far_other, near_high, near_low, nxt, copies):
+def sketch_products(far_own, far_other, near_high, near_low, nxt):
     columns, bond, quarter = near_high.shape
     width = nxt.shape[0]
-    shape = jax.ShapeDtypeStruct((width, columns, quarter), BF16)
+    shape = jax.ShapeDtypeStruct((width // 2, 2 * columns, quarter), BF16)
     blocks = columns * (columns + bond) // 512
     return pl.pallas_call(
         sketch_kernel,
         in_specs=[VMEM] * 5,
         out_specs=[VMEM] * 3,
-        out_shape=[shape, shape, jax.ShapeDtypeStruct((copies, blocks, 4, LANES), F32)],
-        scratch_shapes=[pltpu.VMEM((2, width // 2, columns, quarter), F32)],
+        out_shape=[shape, shape, jax.ShapeDtypeStruct((blocks, 4, LANES), F32)],
+        scratch_shapes=[pltpu.VMEM((width // 2, 2 * columns, quarter), F32)],
         cost_estimate=pl.CostEstimate(flops=2 * columns * bond * width * quarter * 24, bytes_accessed=8 * columns * width * quarter, transcendentals=0),
         compiler_params=params(16),
         name="sketch_products",
     )(far_own, far_other, near_high, near_low, nxt)
 
 
+def pair_kernel(mine_ref, other_ref, out_ref):
+    both = mine_ref[...] + other_ref[...]
+    for i in range(out_ref.shape[0]):
+        out_ref[i] = both
+
+
+def pair_copies(mine, other, copies):
+    return pl.pallas_call(
+        pair_kernel,
+        in_specs=[VMEM] * 2,
+        out_specs=VMEM,
+        out_shape=jax.ShapeDtypeStruct((copies,) + mine.shape, F32),
+        compiler_params=params(8),
+        name="pair_copies",
+    )(mine, other)
+
+
 def basis_kernel(count, sums_ref, high_ref, low_ref, basis_ref, squeezed_ref, square, out, out_sems):
-    width, columns, quarter = high_ref.shape
+    columns, width, quarter = basis_ref.shape
     bond = squeezed_ref.shape[1]
 
     def store(g):
@@ -237,7 +267,8 @@
         square[8 * i:8 * i + 8, columns:columns + bond] = flat[:, first:first + bond]
     matrix = square[...]
     wide = 8 * columns
-    unit = (iota((columns, wide), 1) % columns == iota((columns, wide), 0)).astype(F32)
+    within = iota((columns, wide), 1) % (2 * columns)
+    unit = (within // 8 * 4 + within % 4 == iota((columns, wide), 0)).astype(F32)
     row = iota((columns, LANES), 0)
     roots = jnp.zeros((columns, LANES), F32)
     block = 4
@@ -255,13 +286,13 @@
     squeezed_ref[...] = (matrix * roots)[:, columns:columns + bond] / count ** 0.5
     inverse = unit * jnp.concatenate([roots] * (wide // LANES), axis=1)
     spread = jnp.broadcast_to(inverse[:, None, :], (columns, 8, wide)).reshape(wide, wide)
-    same = iota((wide, wide), 1) // columns == iota((wide, wide), 0) % 8
+    lane = iota((wide, wide), 1)
+    same = lane // (2 * columns) * 2 + lane // 4 % 2 == iota((wide, wide), 0) % 8
     left_high, left_low = halves(jnp.where(same, spread, 0.0))
 
     def group(g, carry):
-        first = pl.multiple_of(8 * g, 8)
-        high = high_ref[pl.ds(first, 8)].reshape(wide, quarter)
-        low = low_ref[pl.ds(first, 8)].reshape(wide, quarter)
+        high = high_ref[pl.ds(4 * g, 4)].reshape(wide, quarter)
+        low = low_ref[pl.ds(4 * g, 4)].reshape(wide, quarter)
         result = jnp.dot(left_high, high, preferred_element_type=F32)
         result += jnp.dot(left_low, high, preferred_element_type=F32)
         result += jnp.dot(left_high, low, preferred_element_type=F32)
@@ -274,7 +305,8 @@
 
 
 def basis_of(sums, high, low, bond, count):
-    width, columns, quarter = high.shape
+    pairs, doubled, quarter = high.shape
+    width, columns = 2 * pairs, doubled // 2
     return pl.pallas_call(
         functools.partial(basis_kernel, float(count)),
         in_specs=[VMEM] * 3,
@@ -307,12 +339,15 @@
     partial = jnp.pad(partial, ((0, each * rows - width // 2), (0, 0), (0, 0))).reshape(rows, each, own, LANES)
     parts = lax.all_to_all(partial, "rows", 0, 0)
     parities = [[i for i in range(devices) if i % 2 == parity] for parity in range(2)]
-    pieces = lax.all_to_all(piece_copies(parts, devices // 2), BOTH, 0, 0, axis_index_groups=parities)
+    pieces = lax.all_to_all(piece_copies(parts, devices // 2, bond), BOTH, 0, 0, axis_index_groups=parities)
     far_own = pieces.reshape(rows, cols // 2, each, own, LANES)
-    far_other = lax.ppermute(far_own, "cols", [(i, i ^ 1) for i in range(cols)])
+    swap = [(i, i ^ 1) for i in range(cols)]
+    far_other = lax.ppermute(far_own, "cols", swap)
     near_high, near_low = near_sums(sketch_leg.T, a_own)
-    high, low, sums = sketch_products(far_own, far_other, near_high, near_low, nxt, devices)
-    basis, squeezed = basis_of(lax.all_to_all(sums, BOTH, 0, 0), high, low, bond, count)
+    high, low, sums = sketch_products(far_own, far_other, near_high, near_low, nxt)
+    sums = pair_copies(sums, lax.ppermute(sums, "cols", swap), devices // 2)
+    sums = lax.all_to_all(sums, BOTH, 0, 0, axis_index_groups=parities)
+    basis, squeezed = basis_of(sums, high, low, bond, count)
     return jnp.transpose(basis, (0, 2, 1)), squeezed
 
 

time: 58.1 us -> 56.4 us (0.971)
  blocking collectives: 39.7 us -> 36.9 us
  waiting for transfers between devices: 0.01 us -> 0.83 us
    all_to_all x2, blocking collectives: 25.4 us -> 22.7 us  [the longest x1 11.4 us: per_device(): sums = lax.all_to_all(sums, BOTH, 0, 0, axis_index_groups=parities)]
    ppermute x1 -> x2, waiting for transfers between devices: 0.01 us -> 0.83 us  [the longest x1 0.83 us: per_device(): sums = pair_copies(sums, lax.ppermute(sums, 'cols', swap), devices // 2)]
  transfers between devices with their start and end apart: 1 -> 2, of which waited for: 0 -> 1; matrix products, arithmetic and copies ran while one was open for 0% -> 0% of each run, Pallas kernels for 3% -> 3%
where the time goes in v4:
time: 56.4 us; the launch traced here: 56.1 us
  blocking collectives  36.9 us (65%)
  Pallas kernels  17.2 us (30%)
  waiting for transfers between devices  0.83 us (1%)
  between operations  0.69 us (1%)
    all_to_all x1, blocking collectives, per_device(): parts = lax.all_to_all(partial, 'rows', 0, 0)  14.2 us
    all_to_all x1, blocking collectives, per_device(): sums = lax.all_to_all(sums, BOTH, 0, 0, axis_index_groups=parities)  11.4 us
    all_to_all x1, blocking collectives, per_device(): lax.all_to_all(piece_copies(parts, devices // 2, bond), BOTH, 0, 0, axis_...  11.3 us
    pallas_call x1, Pallas kernels, sketch_products(): pl.pallas_call(sketch_kernel, in_specs=[VMEM] * 5, out_specs=[VMEM] * 3,...  5.52 us
    pallas_call x1, Pallas kernels, basis_of(): pl.pallas_call(functools.partial(basis_kernel, float(count)), in_specs=[V...  5.13 us
    pallas_call x1, Pallas kernels, far_sum(): pl.pallas_call(far_kernel, in_specs=[HBM] * 3, out_specs=[VMEM] * 2, out_...  4.9 us
    pallas_call x1, Pallas kernels, near_sums(): pl.pallas_call(near_kernel, in_specs=[VMEM, VMEM], out_specs=[VMEM, VMEM]...  1.52 us
  transfers between devices with their start and end apart: 2, of which 1 were waited for; matrix products, arithmetic and copies ran while one was open for 0% of the time, Pallas kernels for 3%

profile of v4, /device:TPU:0, one launch (start us, length us, event | category | flops | bytes accessed | tf_op | source)
XLA Modules:
  0.0 56.1 jit_solution(11755502013518030854)
XLA Ops:
  0.6 0.0 copy-start.1
  0.6 4.9 %far_sum.1 = (f32[24,8,128]{2,1,0:T(8,128)S(1)}, bf16[48,48,512]{2,1,0:T(8,128)(2,1)S(1)}) custom-call(bf16[8,2048]{1,0:T(8,128)(2,1)} %bitcast.17, bf16[24,96,2048]{2,1,0:T(8,128)(2,1)} %bitcast.15, bf16[48,48,2048]{2,1,0:T(8,128)(2,1)} %bitcast.16), custom_call_target="tpu_custom_call" | custom-call | flops 75497472 | bytes 9437184 | tf_op jit(solution)/shard_map/far_sum/pallas_call | solution.py:66
  5.5 14.2 %all_to_all.15.parts_ref = f32[8,3,8,128]{3,2,1,0:T(8,128)S(1)} all-to-all(f32[8,3,8,128]{3,2,1,0:T(8,128)S(1)} %bitcast.12), channel_id=1, replica_groups=mesh['rows'=8,'cols'=4] {'rows'}, dimensions={0} | all-to-all | bytes 196608 | tf_op jit(solution)/shard_map/all_to_all | solution.py:340
  19.8 0.1 piece_copies.1
  19.9 0.0 copy-start
  19.9 11.3 %all_to_all.16 = f32[16,3,8,128]{3,2,1,0:T(8,128)S(1)} all-to-all(f32[16,3,8,128]{3,2,1,0:T(8,128)S(1)} %piece_copies.1), channel_id=1, replica_groups={{0,2,4,6,8,10,12,14,16,18,20,22,24,26,28,30},{1,3,5,7,9,11,13,15,17,19,..., dimensions={0} | all-to-all | bytes 393216 | tf_op jit(solution)/shard_map/all_to_all | solution.py:342
  31.2 0.0 collective-permute-start
  31.2 0.0 copy-done.1
  31.2 1.5 %near_sums.1 = (bf16[32,48,512]{2,1,0:T(8,128)(2,1)S(1)}, bf16[32,48,512]{2,1,0:T(8,128)(2,1)S(1)}) custom-call(bf16[32,48]{1,0:T(8,128)(2,1)S(1)} %bitcast.14, bf16[48,48,512]{2,1,0:T(8,128)(2,1)S(1)} %get-tuple-element.12.a_ref), custom_call_target="tpu_custom_call" | custom-call | flops 1207959552 | bytes 2359296 | tf_op jit(solution)/shard_map/near_sums/pallas_call | solution.py:105
  32.7 0.0 collective-permute-done.other_ref
  32.7 0.0 copy-done
  32.7 5.5 %sketch_products.1 = (bf16[24,64,512]{2,1,0:T(8,128)(2,1)S(1)}, bf16[24,64,512]{2,1,0:T(8,128)(2,1)S(1)}, f32[5,4,128]{2,1,0:T(4,128)S(1)}) custom-call(f32[8,2,3,8,128]{4,3,2,1,0:T(8,128)S(1)} %bitcast.11, f32[8,2,3,8,128]{4,3,2,1,0:T(8,128)S(1)} %collective-permute-done.other_ref, bf16[32,48,512]{2,1,0:T(8,128)(2,1)S(1)} %get-tuple-element.13.near_high_ref, ...), custom_call_target="tpu_custom_call" | custom-call | flops 1811939328 | bytes 6291456 | tf_op jit(solution)/shard_map/sketch_products/pallas_call | solution.py:225
  38.2 0.5 collective-permute-start.1
  38.8 0.8 %collective-permute-done.1.other_ref = f32[5,4,128]{2,1,0:T(4,128)S(1)} collective-permute-done((f32[5,4,128]{2,1,0:T(4,128)S(1)}, f32[5,4,128]{2,1,0:T(4,128)S(1)}, u32[]{:S(2)}, u32[]{:S(2)}) %collective-permute-start.1) | collective-permute-done | bytes 10272 | tf_op jit(solution)/shard_map/ppermute | solution.py:348
  39.6 11.4 %all_to_all.17.sums_ref = f32[16,5,4,128]{3,2,1,0:T(4,128)S(1)} all-to-all(f32[16,5,4,128]{3,2,1,0:T(4,128)S(1)} %pair_copies.1), channel_id=1, replica_groups={{0,2,4,6,8,10,12,14,16,18,20,22,24,26,28,30},{1,3,5,7,9,11,13,15,17,19,..., dimensions={0} | all-to-all | bytes 327680 | tf_op jit(solution)/shard_map/all_to_all | solution.py:349
  51.0 5.1 %basis_of.1 = (f32[32,48,512]{2,1,0:T(8,128)}, f32[32,48]{1,0:T(8,128)}) custom-call(f32[16,5,4,128]{3,2,1,0:T(4,128)S(1)} %all_to_all.17.sums_ref, bf16[24,64,512]{2,1,0:T(8,128)(2,1)S(1)} %get-tuple-element.16.high_ref, bf16[24,64,512]{2,1,0:T(8,128)(2,1)S(1)} %get-tuple-element.17.low_ref), custom_call_target="tpu_custom_call" | custom-call | flops 1207959552 | bytes 3145728 | tf_op jit(solution)/shard_map/basis_of/pallas_call | solution.py:310
  (1 shorter events, 0.0 us)
Async XLA Ops:
  0.6 30.5 %copy-start.1 = (bf16[48,32]{0,1:T(8,128)(2,1)S(1)}, bf16[48,32]{0,1:T(8,128)(2,1)}, u32[]{:S(2)}) copy-start(bf16[48,32]{0,1:T(8,128)(2,1)} %param.8) | copy-start | bytes 9220
  19.9 12.8 %copy-start = (bf16[512,48,48]{0,2,1:T(8,128)(2,1)S(1)}, bf16[512,48,48]{0,2,1:T(8,128)(2,1)}, u32[]{:S(2)}) copy-start(bf16[512,48,48]{0,2,1:T(8,128)(2,1)} %param.7) | copy-start | bytes 7077892
  31.2 1.5 %collective-permute-start = (f32[8,2,3,8,128]{4,3,2,1,0:T(8,128)S(1)}, f32[8,2,3,8,128]{4,3,2,1,0:T(8,128)S(1)}, u32[]{:S(2)}, u32[]{:S(2)}) collective-permute-start(f32[8,2,3,8,128]{4,3,2,1,0:T(8,128)S(1)} %bitcast.10), channel_id=1, source_target_pairs={{0,1},{1,0},{2,3},{3,2},{4,5},{5,4},{6,7},{7,6},{8,9},{9,8},{10,11... | collective-permute-start | bytes 589832 | tf_op jit(solution)/shard_map/ppermute | solution.py:345
  38.2 1.4 %collective-permute-start.1 = (f32[5,4,128]{2,1,0:T(4,128)S(1)}, f32[5,4,128]{2,1,0:T(4,128)S(1)}, u32[]{:S(2)}, u32[]{:S(2)}) collective-permute-start(f32[5,4,128]{2,1,0:T(4,128)S(1)} %get-tuple-element.15.mine_ref), channel_id=1, source_target_pairs={{0,1},{1,0},{2,3},{3,2},{4,5},{5,4},{6,7},{7,6},{8,9},{9,8},{10,11... | collective-permute-start | bytes 30728 | tf_op jit(solution)/shard_map/ppermute | solution.py:348

commit v5 on v4

--- a/solution.py
+++ b/solution.py
@@ -136,7 +136,7 @@
     )(parts)
 
 
-def sketch_kernel(own_ref, other_ref, near_high_ref, near_low_ref, next_ref, high_ref, low_ref, sums_ref, sketch):
+def sketch_kernel(own_ref, other_ref, near_high_ref, near_low_ref, next_ref, high_ref, low_ref, sums_ref, sketch, wide_ref):
     groups, own = own_ref.shape[1], own_ref.shape[3]
     columns, bond, quarter = near_high_ref.shape
     pairs = sketch.shape[0]
@@ -147,25 +147,28 @@
     keep = [(iota((LANES, wide), 0) == lane + half * bond).astype(BF16) for half in range(2)]
     same = iota((pairs * own, wide), 1) // bond == iota((pairs * own, wide), 0) % part
 
-    def group(far_ref, odd, g, carry):
+    def widen(far_ref, odd, g):
         far = halves(far_ref[:, g].reshape(-1, LANES)[:pairs * own])
         for half in range(2):
-            spread = [jnp.dot(piece, keep[half], preferred_element_type=F32) for piece in far]
-            high, low = (jnp.where(same, value, 0.0).astype(BF16) for value in spread)
             block = 2 * (2 * g + odd) + half
-            near_high = near_high_ref[pl.ds(block * part, part)].reshape(wide, quarter)
-            near_low = near_low_ref[pl.ds(block * part, part)].reshape(wide, quarter)
-            both = jnp.dot(jnp.concatenate([high, low], axis=0), near_high, preferred_element_type=F32)
-            result = both[:pairs * own] + both[pairs * own:] + jnp.dot(high, near_low, preferred_element_type=F32)
-            sketch[:, pl.ds(pl.multiple_of(block * own, own), own), :] = result.reshape(pairs, own, quarter)
-        return carry
-
-    lax.fori_loop(0, groups, functools.partial(group, own_ref, parity), 0)
-    lax.fori_loop(0, groups, functools.partial(group, other_ref, 1 - parity), 0)
+            for i, piece in enumerate(far):
+                value = jnp.dot(piece, keep[half], preferred_element_type=F32)
+                wide_ref[block, pl.ds(i * pairs * own, pairs * own), :] = jnp.where(same, value, 0.0).astype(BF16)
+
+    for g in range(groups):
+        widen(own_ref, parity, g)
+        widen(other_ref, 1 - parity, g)
+    for block in range(columns // part):
+        near_high = near_high_ref[block * part:(block + 1) * part].reshape(wide, quarter)
+        near_low = near_low_ref[block * part:(block + 1) * part].reshape(wide, quarter)
+        both = jnp.dot(wide_ref[block], near_high, preferred_element_type=F32)
+        cross = jnp.dot(wide_ref[block, :pairs * own, :], near_low, preferred_element_type=F32)
+        result = both[:pairs * own] + both[pairs * own:] + cross
+        sketch[:, block * own:(block + 1) * own, :] = result.reshape(pairs, own, quarter)
 
     def products(i, total):
-        for step in range(4):
-            pair = 4 * i + step
+        for step in range(pairs // 2):
+            pair = pairs // 2 * i + step
             high, low = halves(sketch[pair])
             high_ref[pair] = high
             low_ref[pair] = low
@@ -175,7 +178,7 @@
 
     doubled = 2 * columns
     rows = doubled + 2 * bond
-    total = lax.fori_loop(0, pairs // 4, products, jnp.zeros((rows, LANES), F32))
+    total = lax.fori_loop(0, 2, products, jnp.zeros((rows, LANES), F32))
     row, lane = iota((rows, LANES), 0), iota((rows, LANES), 1)
     row_y = jnp.where(row < doubled, row // part % 2, (row >= doubled + bond).astype(jnp.int32))
     total = jnp.where(row_y == lane // part % 2, total, 0.0)
@@ -219,7 +222,7 @@
 
 def sketch_products(far_own, far_other, near_high, near_low, nxt):
     columns, bond, quarter = near_high.shape
-    width = nxt.shape[0]
+    width, own = nxt.shape[0], far_own.shape[3]
     shape = jax.ShapeDtypeStruct((width // 2, 2 * columns, quarter), BF16)
     blocks = columns * (columns + bond) // 512
     return pl.pallas_call(
@@ -227,7 +230,10 @@
         in_specs=[VMEM] * 5,
         out_specs=[VMEM] * 3,
         out_shape=[shape, shape, jax.ShapeDtypeStruct((blocks, 4, LANES), F32)],
-        scratch_shapes=[pltpu.VMEM((width // 2, 2 * columns, quarter), F32)],
+        scratch_shapes=[
+            pltpu.VMEM((width // 2, 2 * columns, quarter), F32),
+            pltpu.VMEM((2 * columns // own, own * width, own // 2 * bond), BF16),
+        ],
         cost_estimate=pl.CostEstimate(flops=2 * columns * bond * width * quarter * 24, bytes_accessed=8 * columns * width * quarter, transcendentals=0),
         compiler_params=params(16),
         name="sketch_products",
@@ -300,7 +306,7 @@
         store(g).start()
         return carry
 
-    lax.fori_loop(0, width // 8, group, 0)
+    lax.fori_loop(0, width // 8, group, 0, unroll=True)
     lax.fori_loop(0, width // 8, lambda g, carry: (store(g).wait(), carry)[1], 0)
 
 

time: 56.4 us -> 53.6 us (0.950)
  Pallas kernels: 17.2 us -> 14.4 us
    pallas_call x1, Pallas kernels: 5.52 us -> 3.71 us  [sketch_products(): pl.pallas_call(sketch_kernel, in_specs=[VMEM] * 5, out_specs=[VMEM] * 3,...]
    pallas_call x1, Pallas kernels: 5.13 us -> 4.18 us  [basis_of(): pl.pallas_call(functools.partial(basis_kernel, float(count)), in_specs=[V...]
where the time goes in v5:
time: 53.6 us; the launch traced here: 53.4 us
  blocking collectives  36.9 us (69%)
  Pallas kernels  14.4 us (27%)
  waiting for transfers between devices  0.83 us (2%)
  between operations  0.69 us (1%)
    all_to_all x1, blocking collectives, per_device(): parts = lax.all_to_all(partial, 'rows', 0, 0)  14.2 us
    all_to_all x1, blocking collectives, per_device(): sums = lax.all_to_all(sums, BOTH, 0, 0, axis_index_groups=parities)  11.4 us
    all_to_all x1, blocking collectives, per_device(): lax.all_to_all(piece_copies(parts, devices // 2, bond), BOTH, 0, 0, axis_...  11.3 us
    pallas_call x1, Pallas kernels, far_sum(): pl.pallas_call(far_kernel, in_specs=[HBM] * 3, out_specs=[VMEM] * 2, out_...  4.9 us
    pallas_call x1, Pallas kernels, basis_of(): pl.pallas_call(functools.partial(basis_kernel, float(count)), in_specs=[V...  4.18 us
    pallas_call x1, Pallas kernels, sketch_products(): pl.pallas_call(sketch_kernel, in_specs=[VMEM] * 5, out_specs=[VMEM] * 3,...  3.71 us
    pallas_call x1, Pallas kernels, near_sums(): pl.pallas_call(near_kernel, in_specs=[VMEM, VMEM], out_specs=[VMEM, VMEM]...  1.52 us
  transfers between devices with their start and end apart: 2, of which 1 were waited for; matrix products, arithmetic and copies ran while one was open for 0% of the time, Pallas kernels for 3%

profile of v5, /device:TPU:0, one launch (start us, length us, event | category | flops | bytes accessed | tf_op | source)
XLA Modules:
  0.0 53.4 jit_solution(16953096238056938153)
XLA Ops:
  0.6 0.0 copy-start.1
  0.6 4.9 %far_sum.1 = (f32[24,8,128]{2,1,0:T(8,128)S(1)}, bf16[48,48,512]{2,1,0:T(8,128)(2,1)S(1)}) custom-call(bf16[8,2048]{1,0:T(8,128)(2,1)} %bitcast.17, bf16[24,96,2048]{2,1,0:T(8,128)(2,1)} %bitcast.15, bf16[48,48,2048]{2,1,0:T(8,128)(2,1)} %bitcast.16), custom_call_target="tpu_custom_call" | custom-call | flops 75497472 | bytes 9437184 | tf_op jit(solution)/shard_map/far_sum/pallas_call | solution.py:66
  5.5 14.2 %all_to_all.15.parts_ref = f32[8,3,8,128]{3,2,1,0:T(8,128)S(1)} all-to-all(f32[8,3,8,128]{3,2,1,0:T(8,128)S(1)} %bitcast.12), channel_id=1, replica_groups=mesh['rows'=8,'cols'=4] {'rows'}, dimensions={0} | all-to-all | bytes 196608 | tf_op jit(solution)/shard_map/all_to_all | solution.py:346
  19.8 0.1 piece_copies.1
  19.9 0.0 copy-start
  19.9 11.3 %all_to_all.16 = f32[16,3,8,128]{3,2,1,0:T(8,128)S(1)} all-to-all(f32[16,3,8,128]{3,2,1,0:T(8,128)S(1)} %piece_copies.1), channel_id=1, replica_groups={{0,2,4,6,8,10,12,14,16,18,20,22,24,26,28,30},{1,3,5,7,9,11,13,15,17,19,..., dimensions={0} | all-to-all | bytes 393216 | tf_op jit(solution)/shard_map/all_to_all | solution.py:348
  31.2 0.0 collective-permute-start
  31.2 0.0 copy-done.1
  31.2 1.5 %near_sums.1 = (bf16[32,48,512]{2,1,0:T(8,128)(2,1)S(1)}, bf16[32,48,512]{2,1,0:T(8,128)(2,1)S(1)}) custom-call(bf16[32,48]{1,0:T(8,128)(2,1)S(1)} %bitcast.14, bf16[48,48,512]{2,1,0:T(8,128)(2,1)S(1)} %get-tuple-element.12.a_ref), custom_call_target="tpu_custom_call" | custom-call | flops 1207959552 | bytes 2359296 | tf_op jit(solution)/shard_map/near_sums/pallas_call | solution.py:105
  32.7 0.0 collective-permute-done.other_ref
  32.7 0.0 copy-done
  32.7 3.7 %sketch_products.1 = (bf16[24,64,512]{2,1,0:T(8,128)(2,1)S(1)}, bf16[24,64,512]{2,1,0:T(8,128)(2,1)S(1)}, f32[5,4,128]{2,1,0:T(4,128)S(1)}) custom-call(f32[8,2,3,8,128]{4,3,2,1,0:T(8,128)S(1)} %bitcast.11, f32[8,2,3,8,128]{4,3,2,1,0:T(8,128)S(1)} %collective-permute-done.other_ref, bf16[32,48,512]{2,1,0:T(8,128)(2,1)S(1)} %get-tuple-element.13.near_high_ref, ...), custom_call_target="tpu_custom_call" | custom-call | flops 1811939328 | bytes 6291456 | tf_op jit(solution)/shard_map/sketch_products/pallas_call | solution.py:228
  36.4 0.5 collective-permute-start.1
  37.0 0.8 %collective-permute-done.1.other_ref = f32[5,4,128]{2,1,0:T(4,128)S(1)} collective-permute-done((f32[5,4,128]{2,1,0:T(4,128)S(1)}, f32[5,4,128]{2,1,0:T(4,128)S(1)}, u32[]{:S(2)}, u32[]{:S(2)}) %collective-permute-start.1) | collective-permute-done | bytes 10272 | tf_op jit(solution)/shard_map/ppermute | solution.py:354
  37.8 11.4 %all_to_all.17.sums_ref = f32[16,5,4,128]{3,2,1,0:T(4,128)S(1)} all-to-all(f32[16,5,4,128]{3,2,1,0:T(4,128)S(1)} %pair_copies.1), channel_id=1, replica_groups={{0,2,4,6,8,10,12,14,16,18,20,22,24,26,28,30},{1,3,5,7,9,11,13,15,17,19,..., dimensions={0} | all-to-all | bytes 327680 | tf_op jit(solution)/shard_map/all_to_all | solution.py:355
  49.2 4.2 %basis_of.1 = (f32[32,48,512]{2,1,0:T(8,128)}, f32[32,48]{1,0:T(8,128)}) custom-call(f32[16,5,4,128]{3,2,1,0:T(4,128)S(1)} %all_to_all.17.sums_ref, bf16[24,64,512]{2,1,0:T(8,128)(2,1)S(1)} %get-tuple-element.16.high_ref, bf16[24,64,512]{2,1,0:T(8,128)(2,1)S(1)} %get-tuple-element.17.low_ref), custom_call_target="tpu_custom_call" | custom-call | flops 1207959552 | bytes 3145728 | tf_op jit(solution)/shard_map/basis_of/pallas_call | solution.py:316
  (1 shorter events, 0.0 us)
Async XLA Ops:
  0.6 30.5 %copy-start.1 = (bf16[48,32]{0,1:T(8,128)(2,1)S(1)}, bf16[48,32]{0,1:T(8,128)(2,1)}, u32[]{:S(2)}) copy-start(bf16[48,32]{0,1:T(8,128)(2,1)} %param.8) | copy-start | bytes 9220
  19.9 12.8 %copy-start = (bf16[512,48,48]{0,2,1:T(8,128)(2,1)S(1)}, bf16[512,48,48]{0,2,1:T(8,128)(2,1)}, u32[]{:S(2)}) copy-start(bf16[512,48,48]{0,2,1:T(8,128)(2,1)} %param.7) | copy-start | bytes 7077892
  31.2 1.5 %collective-permute-start = (f32[8,2,3,8,128]{4,3,2,1,0:T(8,128)S(1)}, f32[8,2,3,8,128]{4,3,2,1,0:T(8,128)S(1)}, u32[]{:S(2)}, u32[]{:S(2)}) collective-permute-start(f32[8,2,3,8,128]{4,3,2,1,0:T(8,128)S(1)} %bitcast.10), channel_id=1, source_target_pairs={{0,1},{1,0},{2,3},{3,2},{4,5},{5,4},{6,7},{7,6},{8,9},{9,8},{10,11... | collective-permute-start | bytes 589832 | tf_op jit(solution)/shard_map/ppermute | solution.py:351
  36.4 1.4 %collective-permute-start.1 = (f32[5,4,128]{2,1,0:T(4,128)S(1)}, f32[5,4,128]{2,1,0:T(4,128)S(1)}, u32[]{:S(2)}, u32[]{:S(2)}) collective-permute-start(f32[5,4,128]{2,1,0:T(4,128)S(1)} %get-tuple-element.15.mine_ref), channel_id=1, source_target_pairs={{0,1},{1,0},{2,3},{3,2},{4,5},{5,4},{6,7},{7,6},{8,9},{9,8},{10,11... | collective-permute-start | bytes 30728 | tf_op jit(solution)/shard_map/ppermute | solution.py:354

commit v6 on v5

--- a/solution.py
+++ b/solution.py
@@ -277,7 +277,7 @@
     unit = (within // 8 * 4 + within % 4 == iota((columns, wide), 0)).astype(F32)
     row = iota((columns, LANES), 0)
     roots = jnp.zeros((columns, LANES), F32)
-    block = 4
+    block = 16
     for first in range(0, columns, block):
         cols = [jnp.broadcast_to(matrix[:, first + j:first + j + 1], (columns, LANES)) for j in range(block)]
         for j in range(block):

time: 53.6 us -> 53.1 us (level)
    pallas_call x1, Pallas kernels: 4.18 us -> 3.63 us  [basis_of(): pl.pallas_call(functools.partial(basis_kernel, float(count)), in_specs=[V...]
where the time goes in v6:
time: 53.1 us; the launch traced here: 52.8 us
  blocking collectives  36.9 us (69%)
  Pallas kernels  13.9 us (26%)
  waiting for transfers between devices  0.83 us (2%)
  between operations  0.69 us (1%)
    all_to_all x1, blocking collectives, per_device(): parts = lax.all_to_all(partial, 'rows', 0, 0)  14.2 us
    all_to_all x1, blocking collectives, per_device(): sums = lax.all_to_all(sums, BOTH, 0, 0, axis_index_groups=parities)  11.4 us
    all_to_all x1, blocking collectives, per_device(): lax.all_to_all(piece_copies(parts, devices // 2, bond), BOTH, 0, 0, axis_...  11.3 us
    pallas_call x1, Pallas kernels, far_sum(): pl.pallas_call(far_kernel, in_specs=[HBM] * 3, out_specs=[VMEM] * 2, out_...  4.9 us
    pallas_call x1, Pallas kernels, sketch_products(): pl.pallas_call(sketch_kernel, in_specs=[VMEM] * 5, out_specs=[VMEM] * 3,...  3.71 us
    pallas_call x1, Pallas kernels, basis_of(): pl.pallas_call(functools.partial(basis_kernel, float(count)), in_specs=[V...  3.63 us
    pallas_call x1, Pallas kernels, near_sums(): pl.pallas_call(near_kernel, in_specs=[VMEM, VMEM], out_specs=[VMEM, VMEM]...  1.52 us
  transfers between devices with their start and end apart: 2, of which 1 were waited for; matrix products, arithmetic and copies ran while one was open for 0% of the time, Pallas kernels for 3%

profile of v6, /device:TPU:0, one launch (start us, length us, event | category | flops | bytes accessed | tf_op | source)
XLA Modules:
  0.0 52.8 jit_solution(2398388073904139699)
XLA Ops:
  0.6 0.0 copy-start.1
  0.6 4.9 %far_sum.1 = (f32[24,8,128]{2,1,0:T(8,128)S(1)}, bf16[48,48,512]{2,1,0:T(8,128)(2,1)S(1)}) custom-call(bf16[8,2048]{1,0:T(8,128)(2,1)} %bitcast.17, bf16[24,96,2048]{2,1,0:T(8,128)(2,1)} %bitcast.15, bf16[48,48,2048]{2,1,0:T(8,128)(2,1)} %bitcast.16), custom_call_target="tpu_custom_call" | custom-call | flops 75497472 | bytes 9437184 | tf_op jit(solution)/shard_map/far_sum/pallas_call | solution.py:66
  5.5 14.2 %all_to_all.15.parts_ref = f32[8,3,8,128]{3,2,1,0:T(8,128)S(1)} all-to-all(f32[8,3,8,128]{3,2,1,0:T(8,128)S(1)} %bitcast.12), channel_id=1, replica_groups=mesh['rows'=8,'cols'=4] {'rows'}, dimensions={0} | all-to-all | bytes 196608 | tf_op jit(solution)/shard_map/all_to_all | solution.py:346
  19.8 0.1 piece_copies.1
  19.9 0.0 copy-start
  19.9 11.3 %all_to_all.16 = f32[16,3,8,128]{3,2,1,0:T(8,128)S(1)} all-to-all(f32[16,3,8,128]{3,2,1,0:T(8,128)S(1)} %piece_copies.1), channel_id=1, replica_groups={{0,2,4,6,8,10,12,14,16,18,20,22,24,26,28,30},{1,3,5,7,9,11,13,15,17,19,..., dimensions={0} | all-to-all | bytes 393216 | tf_op jit(solution)/shard_map/all_to_all | solution.py:348
  31.2 0.0 collective-permute-start
  31.2 0.0 copy-done.1
  31.2 1.5 %near_sums.1 = (bf16[32,48,512]{2,1,0:T(8,128)(2,1)S(1)}, bf16[32,48,512]{2,1,0:T(8,128)(2,1)S(1)}) custom-call(bf16[32,48]{1,0:T(8,128)(2,1)S(1)} %bitcast.14, bf16[48,48,512]{2,1,0:T(8,128)(2,1)S(1)} %get-tuple-element.12.a_ref), custom_call_target="tpu_custom_call" | custom-call | flops 1207959552 | bytes 2359296 | tf_op jit(solution)/shard_map/near_sums/pallas_call | solution.py:105
  32.7 0.0 collective-permute-done.other_ref
  32.7 0.0 copy-done
  32.7 3.7 %sketch_products.1 = (bf16[24,64,512]{2,1,0:T(8,128)(2,1)S(1)}, bf16[24,64,512]{2,1,0:T(8,128)(2,1)S(1)}, f32[5,4,128]{2,1,0:T(4,128)S(1)}) custom-call(f32[8,2,3,8,128]{4,3,2,1,0:T(8,128)S(1)} %bitcast.11, f32[8,2,3,8,128]{4,3,2,1,0:T(8,128)S(1)} %collective-permute-done.other_ref, bf16[32,48,512]{2,1,0:T(8,128)(2,1)S(1)} %get-tuple-element.13.near_high_ref, ...), custom_call_target="tpu_custom_call" | custom-call | flops 1811939328 | bytes 6291456 | tf_op jit(solution)/shard_map/sketch_products/pallas_call | solution.py:228
  36.4 0.5 %collective-permute-start.1 = (f32[5,4,128]{2,1,0:T(4,128)S(1)}, f32[5,4,128]{2,1,0:T(4,128)S(1)}, u32[]{:S(2)}, u32[]{:S(2)}) collective-permute-start(f32[5,4,128]{2,1,0:T(4,128)S(1)} %get-tuple-element.15.mine_ref), channel_id=1, source_target_pairs={{0,1},{1,0},{2,3},{3,2},{4,5},{5,4},{6,7},{7,6},{8,9},{9,8},{10,11... | collective-permute-start | bytes 30728 | tf_op jit(solution)/shard_map/ppermute | solution.py:354
  37.0 0.8 %collective-permute-done.1.other_ref = f32[5,4,128]{2,1,0:T(4,128)S(1)} collective-permute-done((f32[5,4,128]{2,1,0:T(4,128)S(1)}, f32[5,4,128]{2,1,0:T(4,128)S(1)}, u32[]{:S(2)}, u32[]{:S(2)}) %collective-permute-start.1) | collective-permute-done | bytes 10272 | tf_op jit(solution)/shard_map/ppermute | solution.py:354
  37.8 11.4 %all_to_all.17.sums_ref = f32[16,5,4,128]{3,2,1,0:T(4,128)S(1)} all-to-all(f32[16,5,4,128]{3,2,1,0:T(4,128)S(1)} %pair_copies.1), channel_id=1, replica_groups={{0,2,4,6,8,10,12,14,16,18,20,22,24,26,28,30},{1,3,5,7,9,11,13,15,17,19,..., dimensions={0} | all-to-all | bytes 327680 | tf_op jit(solution)/shard_map/all_to_all | solution.py:355
  49.2 3.6 %basis_of.1 = (f32[32,48,512]{2,1,0:T(8,128)}, f32[32,48]{1,0:T(8,128)}) custom-call(f32[16,5,4,128]{3,2,1,0:T(4,128)S(1)} %all_to_all.17.sums_ref, bf16[24,64,512]{2,1,0:T(8,128)(2,1)S(1)} %get-tuple-element.16.high_ref, bf16[24,64,512]{2,1,0:T(8,128)(2,1)S(1)} %get-tuple-element.17.low_ref), custom_call_target="tpu_custom_call" | custom-call | flops 1207959552 | bytes 3145728 | tf_op jit(solution)/shard_map/basis_of/pallas_call | solution.py:316
  (1 shorter events, 0.0 us)
Async XLA Ops:
  0.6 30.5 %copy-start.1 = (bf16[48,32]{0,1:T(8,128)(2,1)S(1)}, bf16[48,32]{0,1:T(8,128)(2,1)}, u32[]{:S(2)}) copy-start(bf16[48,32]{0,1:T(8,128)(2,1)} %param.8) | copy-start | bytes 9220
  19.9 12.8 %copy-start = (bf16[512,48,48]{0,2,1:T(8,128)(2,1)S(1)}, bf16[512,48,48]{0,2,1:T(8,128)(2,1)}, u32[]{:S(2)}) copy-start(bf16[512,48,48]{0,2,1:T(8,128)(2,1)} %param.7) | copy-start | bytes 7077892
  31.2 1.5 %collective-permute-start = (f32[8,2,3,8,128]{4,3,2,1,0:T(8,128)S(1)}, f32[8,2,3,8,128]{4,3,2,1,0:T(8,128)S(1)}, u32[]{:S(2)}, u32[]{:S(2)}) collective-permute-start(f32[8,2,3,8,128]{4,3,2,1,0:T(8,128)S(1)} %bitcast.10), channel_id=1, source_target_pairs={{0,1},{1,0},{2,3},{3,2},{4,5},{5,4},{6,7},{7,6},{8,9},{9,8},{10,11... | collective-permute-start | bytes 589832 | tf_op jit(solution)/shard_map/ppermute | solution.py:351
  36.4 1.4 %collective-permute-start.1 = (f32[5,4,128]{2,1,0:T(4,128)S(1)}, f32[5,4,128]{2,1,0:T(4,128)S(1)}, u32[]{:S(2)}, u32[]{:S(2)}) collective-permute-start(f32[5,4,128]{2,1,0:T(4,128)S(1)} %get-tuple-element.15.mine_ref), channel_id=1, source_target_pairs={{0,1},{1,0},{2,3},{3,2},{4,5},{5,4},{6,7},{7,6},{8,9},{9,8},{10,11... | collective-permute-start | bytes 30728 | tf_op jit(solution)/shard_map/ppermute | solution.py:354

commit v7 on v6

--- a/solution.py
+++ b/solution.py
@@ -185,7 +185,10 @@
     lane, target = iota((LANES, doubled), 0), iota((LANES, doubled), 1)
     column = lane % doubled // own * part + lane % part
     pick = (column == target % columns) & ((target < columns) | (lane >= doubled))
-    packed = jnp.dot(total, pick.astype(F32), preferred_element_type=F32, precision=lax.Precision.HIGHEST)
+    first = total.astype(BF16)
+    thirds = jnp.concatenate([first, *halves(total - first.astype(F32))], axis=0)
+    packed = jnp.dot(thirds, pick.astype(F32).astype(BF16), preferred_element_type=F32)
+    packed = packed[:rows] + packed[rows:2 * rows] + packed[2 * rows:]
     squares = packed[:doubled].reshape(doubled // own, own, doubled)
     squares = squares + pltpu.roll(squares, part, 1)
     upper = iota((own, doubled), 0) < part
@@ -261,8 +264,10 @@
     columns, width, quarter = basis_ref.shape
     bond = squeezed_ref.shape[1]
 
-    def store(g):
-        return pltpu.make_async_copy(out.at[g], basis_ref.at[:, pl.ds(pl.multiple_of(8 * g, 8), 8), :], out_sems.at[g])
+    def store(g, half):
+        part = pl.ds(half * (columns // 2), columns // 2)
+        target = basis_ref.at[part, pl.ds(pl.multiple_of(8 * g, 8), 8), :]
+        return pltpu.make_async_copy(out.at[g, part], target, out_sems.at[half, g])
 
     summed = jnp.sum(sums_ref[...], axis=0)
     flat = unfold([summed[i] for i in range(summed.shape[0])])
@@ -296,18 +301,19 @@
     same = lane // (2 * columns) * 2 + lane // 4 % 2 == iota((wide, wide), 0) % 8
     left_high, left_low = halves(jnp.where(same, spread, 0.0))
 
-    def group(g, carry):
-        high = high_ref[pl.ds(4 * g, 4)].reshape(wide, quarter)
-        low = low_ref[pl.ds(4 * g, 4)].reshape(wide, quarter)
-        result = jnp.dot(left_high, high, preferred_element_type=F32)
-        result += jnp.dot(left_low, high, preferred_element_type=F32)
-        result += jnp.dot(left_high, low, preferred_element_type=F32)
-        out[g] = result.reshape(columns, 8, quarter)
-        store(g).start()
-        return carry
-
-    lax.fori_loop(0, width // 8, group, 0, unroll=True)
-    lax.fori_loop(0, width // 8, lambda g, carry: (store(g).wait(), carry)[1], 0)
+    for g in range(width // 8):
+        high = high_ref[4 * g:4 * g + 4].reshape(wide, quarter)
+        low = low_ref[4 * g:4 * g + 4].reshape(wide, quarter)
+        for half in range(2):
+            rows = slice(half * (wide // 2), (half + 1) * (wide // 2))
+            result = jnp.dot(left_high[rows], high, preferred_element_type=F32)
+            result += jnp.dot(left_low[rows], high, preferred_element_type=F32)
+            result += jnp.dot(left_high[rows], low, preferred_element_type=F32)
+            out[g, half * (columns // 2):(half + 1) * (columns // 2)] = result.reshape(columns // 2, 8, quarter)
+            store(g, half).start()
+    for g in range(width // 8):
+        for half in range(2):
+            store(g, half).wait()
 
 
 def basis_of(sums, high, low, bond, count):
@@ -321,7 +327,7 @@
         scratch_shapes=[
             pltpu.VMEM((columns, LANES), F32),
             pltpu.VMEM((width // 8, columns, 8, quarter), F32),
-            pltpu.SemaphoreType.DMA((width // 8,)),
+            pltpu.SemaphoreType.DMA((2, width // 8)),
         ],
         cost_estimate=pl.CostEstimate(flops=2 * columns * columns * width * quarter * 24, bytes_accessed=4 * columns * width * quarter, transcendentals=0),
         compiler_params=params(16),

time: 53.1 us -> 53 us (level)
  no operation moved by 1% of the time
where the time goes in v7:
time: 53 us; the launch traced here: 52.7 us
  blocking collectives  36.9 us (70%)
  Pallas kernels  13.8 us (26%)
  waiting for transfers between devices  0.83 us (2%)
  between operations  0.69 us (1%)
  starting transfers between devices  0.53 us (1%)
    all_to_all x1, blocking collectives, per_device(): parts = lax.all_to_all(partial, 'rows', 0, 0)  14.2 us
    all_to_all x1, blocking collectives, per_device(): sums = lax.all_to_all(sums, BOTH, 0, 0, axis_index_groups=parities)  11.4 us
    all_to_all x1, blocking collectives, per_device(): lax.all_to_all(piece_copies(parts, devices // 2, bond), BOTH, 0, 0, axis_...  11.3 us
    pallas_call x1, Pallas kernels, far_sum(): pl.pallas_call(far_kernel, in_specs=[HBM] * 3, out_specs=[VMEM] * 2, out_...  4.9 us
    pallas_call x1, Pallas kernels, sketch_products(): pl.pallas_call(sketch_kernel, in_specs=[VMEM] * 5, out_specs=[VMEM] * 3,...  3.67 us
    pallas_call x1, Pallas kernels, basis_of(): pl.pallas_call(functools.partial(basis_kernel, float(count)), in_specs=[V...  3.59 us
    pallas_call x1, Pallas kernels, near_sums(): pl.pallas_call(near_kernel, in_specs=[VMEM, VMEM], out_specs=[VMEM, VMEM]...  1.52 us
  transfers between devices with their start and end apart: 2, of which 1 were waited for; matrix products, arithmetic and copies ran while one was open for 0% of the time, Pallas kernels for 3%

profile of v7, /device:TPU:0, one launch (start us, length us, event | category | flops | bytes accessed | tf_op | source)
XLA Modules:
  0.0 52.7 jit_solution(12911177335278908120)
XLA Ops:
  0.6 0.0 copy-start.1
  0.6 4.9 %far_sum.1 = (f32[24,8,128]{2,1,0:T(8,128)S(1)}, bf16[48,48,512]{2,1,0:T(8,128)(2,1)S(1)}) custom-call(bf16[8,2048]{1,0:T(8,128)(2,1)} %bitcast.17, bf16[24,96,2048]{2,1,0:T(8,128)(2,1)} %bitcast.15, bf16[48,48,2048]{2,1,0:T(8,128)(2,1)} %bitcast.16), custom_call_target="tpu_custom_call" | custom-call | flops 75497472 | bytes 9437184 | tf_op jit(solution)/shard_map/far_sum/pallas_call | solution.py:66
  5.5 14.2 %all_to_all.15.parts_ref = f32[8,3,8,128]{3,2,1,0:T(8,128)S(1)} all-to-all(f32[8,3,8,128]{3,2,1,0:T(8,128)S(1)} %bitcast.12), channel_id=1, replica_groups=mesh['rows'=8,'cols'=4] {'rows'}, dimensions={0} | all-to-all | bytes 196608 | tf_op jit(solution)/shard_map/all_to_all | solution.py:352
  19.8 0.1 piece_copies.1
  19.9 0.0 copy-start
  19.9 11.3 %all_to_all.16 = f32[16,3,8,128]{3,2,1,0:T(8,128)S(1)} all-to-all(f32[16,3,8,128]{3,2,1,0:T(8,128)S(1)} %piece_copies.1), channel_id=1, replica_groups={{0,2,4,6,8,10,12,14,16,18,20,22,24,26,28,30},{1,3,5,7,9,11,13,15,17,19,..., dimensions={0} | all-to-all | bytes 393216 | tf_op jit(solution)/shard_map/all_to_all | solution.py:354
  31.2 0.0 collective-permute-start
  31.2 0.0 copy-done.1
  31.2 1.5 %near_sums.1 = (bf16[32,48,512]{2,1,0:T(8,128)(2,1)S(1)}, bf16[32,48,512]{2,1,0:T(8,128)(2,1)S(1)}) custom-call(bf16[32,48]{1,0:T(8,128)(2,1)S(1)} %bitcast.14, bf16[48,48,512]{2,1,0:T(8,128)(2,1)S(1)} %get-tuple-element.12.a_ref), custom_call_target="tpu_custom_call" | custom-call | flops 1207959552 | bytes 2359296 | tf_op jit(solution)/shard_map/near_sums/pallas_call | solution.py:105
  32.7 0.0 collective-permute-done.other_ref
  32.7 0.0 copy-done
  32.7 3.7 %sketch_products.1 = (bf16[24,64,512]{2,1,0:T(8,128)(2,1)S(1)}, bf16[24,64,512]{2,1,0:T(8,128)(2,1)S(1)}, f32[5,4,128]{2,1,0:T(4,128)S(1)}) custom-call(f32[8,2,3,8,128]{4,3,2,1,0:T(8,128)S(1)} %bitcast.11, f32[8,2,3,8,128]{4,3,2,1,0:T(8,128)S(1)} %collective-permute-done.other_ref, bf16[32,48,512]{2,1,0:T(8,128)(2,1)S(1)} %get-tuple-element.13.near_high_ref, ...), custom_call_target="tpu_custom_call" | custom-call | flops 1811939328 | bytes 6291456 | tf_op jit(solution)/shard_map/sketch_products/pallas_call | solution.py:231
  36.4 0.5 %collective-permute-start.1 = (f32[5,4,128]{2,1,0:T(4,128)S(1)}, f32[5,4,128]{2,1,0:T(4,128)S(1)}, u32[]{:S(2)}, u32[]{:S(2)}) collective-permute-start(f32[5,4,128]{2,1,0:T(4,128)S(1)} %get-tuple-element.15.mine_ref), channel_id=1, source_target_pairs={{0,1},{1,0},{2,3},{3,2},{4,5},{5,4},{6,7},{7,6},{8,9},{9,8},{10,11... | collective-permute-start | bytes 30728 | tf_op jit(solution)/shard_map/ppermute | solution.py:360
  36.9 0.8 %collective-permute-done.1.other_ref = f32[5,4,128]{2,1,0:T(4,128)S(1)} collective-permute-done((f32[5,4,128]{2,1,0:T(4,128)S(1)}, f32[5,4,128]{2,1,0:T(4,128)S(1)}, u32[]{:S(2)}, u32[]{:S(2)}) %collective-permute-start.1) | collective-permute-done | bytes 10272 | tf_op jit(solution)/shard_map/ppermute | solution.py:360
  37.8 11.4 %all_to_all.17.sums_ref = f32[16,5,4,128]{3,2,1,0:T(4,128)S(1)} all-to-all(f32[16,5,4,128]{3,2,1,0:T(4,128)S(1)} %pair_copies.1), channel_id=1, replica_groups={{0,2,4,6,8,10,12,14,16,18,20,22,24,26,28,30},{1,3,5,7,9,11,13,15,17,19,..., dimensions={0} | all-to-all | bytes 327680 | tf_op jit(solution)/shard_map/all_to_all | solution.py:361
  49.2 3.6 %basis_of.1 = (f32[32,48,512]{2,1,0:T(8,128)}, f32[32,48]{1,0:T(8,128)}) custom-call(f32[16,5,4,128]{3,2,1,0:T(4,128)S(1)} %all_to_all.17.sums_ref, bf16[24,64,512]{2,1,0:T(8,128)(2,1)S(1)} %get-tuple-element.16.high_ref, bf16[24,64,512]{2,1,0:T(8,128)(2,1)S(1)} %get-tuple-element.17.low_ref), custom_call_target="tpu_custom_call" | custom-call | flops 1207959552 | bytes 3145728 | tf_op jit(solution)/shard_map/basis_of/pallas_call | solution.py:322
  (1 shorter events, 0.0 us)
Async XLA Ops:
  0.6 30.5 %copy-start.1 = (bf16[48,32]{0,1:T(8,128)(2,1)S(1)}, bf16[48,32]{0,1:T(8,128)(2,1)}, u32[]{:S(2)}) copy-start(bf16[48,32]{0,1:T(8,128)(2,1)} %param.8) | copy-start | bytes 9220
  19.9 12.8 %copy-start = (bf16[512,48,48]{0,2,1:T(8,128)(2,1)S(1)}, bf16[512,48,48]{0,2,1:T(8,128)(2,1)}, u32[]{:S(2)}) copy-start(bf16[512,48,48]{0,2,1:T(8,128)(2,1)} %param.7) | copy-start | bytes 7077892
  31.2 1.5 %collective-permute-start = (f32[8,2,3,8,128]{4,3,2,1,0:T(8,128)S(1)}, f32[8,2,3,8,128]{4,3,2,1,0:T(8,128)S(1)}, u32[]{:S(2)}, u32[]{:S(2)}) collective-permute-start(f32[8,2,3,8,128]{4,3,2,1,0:T(8,128)S(1)} %bitcast.10), channel_id=1, source_target_pairs={{0,1},{1,0},{2,3},{3,2},{4,5},{5,4},{6,7},{7,6},{8,9},{9,8},{10,11... | collective-permute-start | bytes 589832 | tf_op jit(solution)/shard_map/ppermute | solution.py:357
  36.4 1.4 %collective-permute-start.1 = (f32[5,4,128]{2,1,0:T(4,128)S(1)}, f32[5,4,128]{2,1,0:T(4,128)S(1)}, u32[]{:S(2)}, u32[]{:S(2)}) collective-permute-start(f32[5,4,128]{2,1,0:T(4,128)S(1)} %get-tuple-element.15.mine_ref), channel_id=1, source_target_pairs={{0,1},{1,0},{2,3},{3,2},{4,5},{5,4},{6,7},{7,6},{8,9},{9,8},{10,11... | collective-permute-start | bytes 30728 | tf_op jit(solution)/shard_map/ppermute | solution.py:360

commit v8 on v6

--- a/solution.py
+++ b/solution.py
@@ -41,7 +41,7 @@
 
     rows_copy = pltpu.make_async_copy(rows_ref, rows_buf, rows_sem)
     rows_copy.start()
-    ahead = 2
+    ahead = 1
     for c in range(ahead):
         fetch(c).start()
     own_copy = pltpu.make_async_copy(a_ref.at[:, :, pl.ds(start, quarter)], own_ref, own_sem)

time: 53.1 us -> 53 us (level)
  no operation moved by 1% of the time
where the time goes in v8:
time: 53 us; the launch traced here: 52.8 us
  blocking collectives  36.9 us (70%)
  Pallas kernels  13.8 us (26%)
  waiting for transfers between devices  0.83 us (2%)
  between operations  0.69 us (1%)
  starting transfers between devices  0.54 us (1%)
    all_to_all x1, blocking collectives, per_device(): parts = lax.all_to_all(partial, 'rows', 0, 0)  14.2 us
    all_to_all x1, blocking collectives, per_device(): sums = lax.all_to_all(sums, BOTH, 0, 0, axis_index_groups=parities)  11.4 us
    all_to_all x1, blocking collectives, per_device(): lax.all_to_all(piece_copies(parts, devices // 2, bond), BOTH, 0, 0, axis_...  11.3 us
    pallas_call x1, Pallas kernels, far_sum(): pl.pallas_call(far_kernel, in_specs=[HBM] * 3, out_specs=[VMEM] * 2, out_...  4.85 us
    pallas_call x1, Pallas kernels, sketch_products(): pl.pallas_call(sketch_kernel, in_specs=[VMEM] * 5, out_specs=[VMEM] * 3,...  3.71 us
    pallas_call x1, Pallas kernels, basis_of(): pl.pallas_call(functools.partial(basis_kernel, float(count)), in_specs=[V...  3.63 us
    pallas_call x1, Pallas kernels, near_sums(): pl.pallas_call(near_kernel, in_specs=[VMEM, VMEM], out_specs=[VMEM, VMEM]...  1.52 us
  transfers between devices with their start and end apart: 2, of which 1 were waited for; matrix products, arithmetic and copies ran while one was open for 0% of the time, Pallas kernels for 3%

profile of v8, /device:TPU:0, one launch (start us, length us, event | category | flops | bytes accessed | tf_op | source)
XLA Modules:
  0.0 52.8 jit_solution(7633680052678791685)
XLA Ops:
  0.6 0.0 copy-start.1
  0.6 4.8 %far_sum.1 = (f32[24,8,128]{2,1,0:T(8,128)S(1)}, bf16[48,48,512]{2,1,0:T(8,128)(2,1)S(1)}) custom-call(bf16[8,2048]{1,0:T(8,128)(2,1)} %bitcast.17, bf16[24,96,2048]{2,1,0:T(8,128)(2,1)} %bitcast.15, bf16[48,48,2048]{2,1,0:T(8,128)(2,1)} %bitcast.16), custom_call_target="tpu_custom_call" | custom-call | flops 75497472 | bytes 9437184 | tf_op jit(solution)/shard_map/far_sum/pallas_call | solution.py:66
  5.5 14.2 %all_to_all.15.parts_ref = f32[8,3,8,128]{3,2,1,0:T(8,128)S(1)} all-to-all(f32[8,3,8,128]{3,2,1,0:T(8,128)S(1)} %bitcast.12), channel_id=1, replica_groups=mesh['rows'=8,'cols'=4] {'rows'}, dimensions={0} | all-to-all | bytes 196608 | tf_op jit(solution)/shard_map/all_to_all | solution.py:346
  19.7 0.1 piece_copies.1
  19.8 0.0 copy-start
  19.8 11.3 %all_to_all.16 = f32[16,3,8,128]{3,2,1,0:T(8,128)S(1)} all-to-all(f32[16,3,8,128]{3,2,1,0:T(8,128)S(1)} %piece_copies.1), channel_id=1, replica_groups={{0,2,4,6,8,10,12,14,16,18,20,22,24,26,28,30},{1,3,5,7,9,11,13,15,17,19,..., dimensions={0} | all-to-all | bytes 393216 | tf_op jit(solution)/shard_map/all_to_all | solution.py:348
  31.1 0.0 collective-permute-start
  31.1 0.0 copy-done.1
  31.1 1.5 %near_sums.1 = (bf16[32,48,512]{2,1,0:T(8,128)(2,1)S(1)}, bf16[32,48,512]{2,1,0:T(8,128)(2,1)S(1)}) custom-call(bf16[32,48]{1,0:T(8,128)(2,1)S(1)} %bitcast.14, bf16[48,48,512]{2,1,0:T(8,128)(2,1)S(1)} %get-tuple-element.12.a_ref), custom_call_target="tpu_custom_call" | custom-call | flops 1207959552 | bytes 2359296 | tf_op jit(solution)/shard_map/near_sums/pallas_call | solution.py:105
  32.6 0.0 collective-permute-done.other_ref
  32.7 0.0 copy-done
  32.7 3.7 %sketch_products.1 = (bf16[24,64,512]{2,1,0:T(8,128)(2,1)S(1)}, bf16[24,64,512]{2,1,0:T(8,128)(2,1)S(1)}, f32[5,4,128]{2,1,0:T(4,128)S(1)}) custom-call(f32[8,2,3,8,128]{4,3,2,1,0:T(8,128)S(1)} %bitcast.11, f32[8,2,3,8,128]{4,3,2,1,0:T(8,128)S(1)} %collective-permute-done.other_ref, bf16[32,48,512]{2,1,0:T(8,128)(2,1)S(1)} %get-tuple-element.13.near_high_ref, ...), custom_call_target="tpu_custom_call" | custom-call | flops 1811939328 | bytes 6291456 | tf_op jit(solution)/shard_map/sketch_products/pallas_call | solution.py:228
  36.4 0.5 %collective-permute-start.1 = (f32[5,4,128]{2,1,0:T(4,128)S(1)}, f32[5,4,128]{2,1,0:T(4,128)S(1)}, u32[]{:S(2)}, u32[]{:S(2)}) collective-permute-start(f32[5,4,128]{2,1,0:T(4,128)S(1)} %get-tuple-element.15.mine_ref), channel_id=1, source_target_pairs={{0,1},{1,0},{2,3},{3,2},{4,5},{5,4},{6,7},{7,6},{8,9},{9,8},{10,11... | collective-permute-start | bytes 30728 | tf_op jit(solution)/shard_map/ppermute | solution.py:354
  36.9 0.8 %collective-permute-done.1.other_ref = f32[5,4,128]{2,1,0:T(4,128)S(1)} collective-permute-done((f32[5,4,128]{2,1,0:T(4,128)S(1)}, f32[5,4,128]{2,1,0:T(4,128)S(1)}, u32[]{:S(2)}, u32[]{:S(2)}) %collective-permute-start.1) | collective-permute-done | bytes 10272 | tf_op jit(solution)/shard_map/ppermute | solution.py:354
  37.8 11.4 %all_to_all.17.sums_ref = f32[16,5,4,128]{3,2,1,0:T(4,128)S(1)} all-to-all(f32[16,5,4,128]{3,2,1,0:T(4,128)S(1)} %pair_copies.1), channel_id=1, replica_groups={{0,2,4,6,8,10,12,14,16,18,20,22,24,26,28,30},{1,3,5,7,9,11,13,15,17,19,..., dimensions={0} | all-to-all | bytes 327680 | tf_op jit(solution)/shard_map/all_to_all | solution.py:355
  49.1 3.6 %basis_of.1 = (f32[32,48,512]{2,1,0:T(8,128)}, f32[32,48]{1,0:T(8,128)}) custom-call(f32[16,5,4,128]{3,2,1,0:T(4,128)S(1)} %all_to_all.17.sums_ref, bf16[24,64,512]{2,1,0:T(8,128)(2,1)S(1)} %get-tuple-element.16.high_ref, bf16[24,64,512]{2,1,0:T(8,128)(2,1)S(1)} %get-tuple-element.17.low_ref), custom_call_target="tpu_custom_call" | custom-call | flops 1207959552 | bytes 3145728 | tf_op jit(solution)/shard_map/basis_of/pallas_call | solution.py:316
  (1 shorter events, 0.0 us)
Async XLA Ops:
  0.6 30.5 %copy-start.1 = (bf16[48,32]{0,1:T(8,128)(2,1)S(1)}, bf16[48,32]{0,1:T(8,128)(2,1)}, u32[]{:S(2)}) copy-start(bf16[48,32]{0,1:T(8,128)(2,1)} %param.8) | copy-start | bytes 9220
  19.8 12.8 %copy-start = (bf16[512,48,48]{0,2,1:T(8,128)(2,1)S(1)}, bf16[512,48,48]{0,2,1:T(8,128)(2,1)}, u32[]{:S(2)}) copy-start(bf16[512,48,48]{0,2,1:T(8,128)(2,1)} %param.7) | copy-start | bytes 7077892
  31.1 1.5 %collective-permute-start = (f32[8,2,3,8,128]{4,3,2,1,0:T(8,128)S(1)}, f32[8,2,3,8,128]{4,3,2,1,0:T(8,128)S(1)}, u32[]{:S(2)}, u32[]{:S(2)}) collective-permute-start(f32[8,2,3,8,128]{4,3,2,1,0:T(8,128)S(1)} %bitcast.10), channel_id=1, source_target_pairs={{0,1},{1,0},{2,3},{3,2},{4,5},{5,4},{6,7},{7,6},{8,9},{9,8},{10,11... | collective-permute-start | bytes 589832 | tf_op jit(solution)/shard_map/ppermute | solution.py:351
  36.4 1.4 %collective-permute-start.1 = (f32[5,4,128]{2,1,0:T(4,128)S(1)}, f32[5,4,128]{2,1,0:T(4,128)S(1)}, u32[]{:S(2)}, u32[]{:S(2)}) collective-permute-start(f32[5,4,128]{2,1,0:T(4,128)S(1)} %get-tuple-element.15.mine_ref), channel_id=1, source_target_pairs={{0,1},{1,0},{2,3},{3,2},{4,5},{5,4},{6,7},{7,6},{8,9},{9,8},{10,11... | collective-permute-start | bytes 30728 | tf_op jit(solution)/shard_map/ppermute | solution.py:354
